TPU v7x, 128 devices: a whole 4x4x4 slice. The times are simulated.
128 devices in a mesh: seq: 32 (over x, z, core), head: 4 (over y).
Axes of the slice: x: 4, y: 4, z: 4, core: 2. Of those that a mesh axis runs over, the one named last changes fastest.
Arguments:
- inputs: bfloat16 [32768, 4096], P('seq', 'head'), may hold values from -6 to 6
- out_grad: bfloat16 [32768, 4096], P('seq', 'head'), may hold values from -6 to 6
- b_proj: bfloat16 [32768, 128], P('seq'), may hold values from -0.75 to 0.75
- c_proj: bfloat16 [32768, 128], P('seq'), may hold values from -3 to 3
- step_raw: float32 [32768, 64], P('seq', 'head'), may hold values from -3 to 12
- log_rate: float32 [64], P('head'), may hold values from -7 to -1.7
- step_bias: float32 [64], P('head'), may hold values from -7 to -1.6
- skip_gain: float32 [64], P('head'), may hold values from 0.5 to 1.5
- saved_states: float32 [32, 64, 64, 128], P(None, 'seq', 'head'), may hold values from -1.5 to 1.5
- segment_slot: int32 [32], replicated, may hold values from 0 to 31, each once
Outputs:
- grad_inputs: bfloat16 [32768, 4096], P('seq', 'head')
- grad_step_raw: float32 [32768, 64], P('seq', 'head')
- grad_b: float32 [32768, 128], P(('seq', 'head'))
- grad_c: float32 [32768, 128], P(('seq', 'head'))
Inputs may be any that keep to these rules, and one draw needn't show every extreme that they name: `segment_slot`: a permutation of the segments.
All inputs are finite; a program needn't handle non-finite values.
Results may differ from a plain program's by a relative error of at most 0.0012.
Values sent between devices are 32-bit elements; how exact they have to be, the bound alone decides.
No kernel may reach another device: no remote copies, remote signals or barrier semaphores. Data moves between devices by JAX's collectives and lax.ppermute only.
A program may use at most 128 MiB of HBM per device.

v0:
```python
import jax
import jax.numpy as jnp
from jax import lax
from jax.experimental import pallas as pl
from jax.experimental.pallas import tpu as pltpu
from jax.sharding import PartitionSpec as P

f32 = jnp.float32
bf16 = jnp.bfloat16
Q = 128
LOG2E = 1.4426950408889634
HIGHEST = lax.Precision.HIGHEST


def dn(a, b, precision=None):
    return lax.dot_general(
        a, b, (((1,), (0,)), ((), ())), precision=precision, preferred_element_type=f32
    )


def dt(a, b, precision=None):
    return lax.dot_general(
        a, b, (((1,), (1,)), ((), ())), precision=precision, preferred_element_type=f32
    )


def split(value):
    high = value.astype(bf16)
    low = (value - high.astype(f32)).astype(bf16)
    return high, low


def side(*parts):
    return jnp.concatenate(parts, axis=1)


def stack(*parts):
    return jnp.concatenate(parts, axis=0)


def spread(cols, base):
    rows = cols.shape[0]
    first = lax.broadcasted_iota(jnp.int32, (rows, 128), 1) < 64
    parts = []
    for j in range(2):
        left, right = (
            jnp.broadcast_to(cols[:, k : k + 1], (rows, 128))
            for k in (base + 2 * j, base + 2 * j + 1)
        )
        parts.append(jnp.where(first, left, right))
    return side(*parts)


def group_cols(cols, group):
    return pltpu.roll(cols, (128 - 4 * group) % 128, 1)


def head_sums(product):
    rows = []
    for j in range(2):
        turned = product[:, 128 * j : 128 * j + 128].T
        for i in range(2):
            part = turned[64 * i : 64 * i + 64]
            eight = part[0:8]
            for r in range(1, 8):
                eight = eight + part[8 * r : 8 * r + 8]
            rows.append(jnp.sum(eight, axis=0, keepdims=True))
    return stack(*rows)


GROW, SHRINK = 0, 32
LOGCOL, GROW_ALL, SKIP = (16 * q for q in range(3))


def repeater(base, group):
    row = lax.broadcasted_iota(jnp.int32, (128, 256), 0) - (base + 4 * group)
    head = lax.broadcasted_iota(jnp.int32, (128, 256), 1) // 64
    return jnp.where((row == head) | (row == head + 16), 1.0, 0.0).astype(bf16)


def first_kernel(
    slot_ref, raw_ref, rate_ref, bias_ref, skip_ref, dy_ref, b_ref, c_ref, saved_ref,
    sums_ref, cols_ref, scales_ref, info_ref, bt_ref, ct_ref,
    pad_ref,
):
    g = pl.program_id(0)
    blocks = dy_ref.shape[0] // Q

    @pl.when(g == 0)
    def prepare():
        for k in range(saved_ref.shape[0]):
            sums_ref[slot_ref[k], 40:72, :] = saved_ref[k]
        pad_ref[0:8, 0:16] = jnp.broadcast_to(jnp.exp(rate_ref[...]), (8, 16))
        pad_ref[8:16, 0:16] = jnp.broadcast_to(bias_ref[...], (8, 16))
        pad_ref[16:24, 0:16] = jnp.broadcast_to(skip_ref[...], (8, 16))
        small = pad_ref[...].T
        rate, bias, skip = (
            jnp.broadcast_to(small[0:16, k : k + 1], (16, Q)) for k in (0, 8, 16)
        )
        row = lax.broadcasted_iota(jnp.int32, (Q, Q), 0)
        lane = lax.broadcasted_iota(jnp.int32, (Q, Q), 1)
        upper = jnp.where(row <= lane, 1.0, 0.0)
        steps, gates, decays = [], [], []
        for k in range(blocks):
            z = raw_ref[:, k * Q : (k + 1) * Q] + bias
            small_exp = jnp.exp(-jnp.abs(z))
            step = jnp.maximum(z, 0.0) + jnp.log1p(small_exp)
            gates.append(jnp.where(z >= 0.0, 1.0, small_exp) / (1.0 + small_exp))
            steps.append(step)
            decays.append(-rate * step * LOG2E)
        sums = dn(stack(*decays), upper, HIGHEST)
        logs = [sums[16 * k : 16 * k + 16] for k in range(blocks)]
        ends = [log[:, Q - 1 : Q] for log in logs]
        so_far = jnp.zeros_like(ends[0])
        fill = jnp.zeros((80, Q), f32)
        fill_scales = jnp.zeros((64, Q), f32)
        for k in range(blocks):
            log, step = logs[k], steps[k]
            cols_ref[k * Q : (k + 1) * Q, :] = stack(
                log - jnp.log(step) * LOG2E,
                jnp.exp2(log + so_far),
                skip,
                fill,
            ).T
            grow, shrink = jnp.exp2(log), step * jnp.exp2(ends[k] - log)
            grow_high, shrink_high = (
                part.astype(bf16).astype(f32) for part in (grow, shrink)
            )
            scales_ref[k * Q : (k + 1) * Q, :] = stack(
                grow_high, grow - grow_high, shrink_high, shrink - shrink_high, fill_scales
            ).T.astype(bf16)
            so_far = so_far + ends[k]
            for r in range(4):
                four = slice(4 * r, 4 * r + 4)
                info_ref[r, :, k * Q : (k + 1) * Q] = stack(
                    log[four], step[four], gates[k][four], rate[four]
                )
            ct_ref[k] = c_ref[k * Q : (k + 1) * Q, :].astype(f32).T.astype(bf16)
            bt_ref[k] = b_ref[k * Q : (k + 1) * Q, :].astype(f32).T.astype(bf16)
        zero_rows = jnp.zeros((4, 128), f32)
        ends_row = []
        for r in range(4):
            last = spread(cols_ref[blocks * Q - 8 : blocks * Q, :], GROW_ALL + 4 * r)[7:8, :]
            ends_row += [last[:, 0:128], last[:, 128:256]]
        for half in range(2):
            tile = stack(*ends_row[4 * half : 4 * half + 4], zero_rows)
            for i in range(16):
                sums_ref[2 * i + half, 32:40, :] = tile

    total = jnp.zeros((128, 256), f32)
    before = None
    grow_to = repeater(GROW, g)
    for k in range(blocks):
        rows = slice(k * Q, (k + 1) * Q)
        grow = dn(scales_ref[rows, :], grow_to)
        high, low = split(dy_ref[rows, :].astype(f32) * grow)
        ct = ct_ref[k]
        delta = dn(side(ct, ct), stack(high, low))
        end = grow[Q - 1 : Q, :]
        total = delta if k == 0 else total + before * delta
        before = end if k == 0 else before * end
    at = pl.ds(pl.multiple_of((g % 2) * 16, 16), 16)
    for i in range(16):
        part = total[8 * i : 8 * i + 8]
        sums_ref[2 * i + g // 2, at, :] = stack(part[:, 0:128], part[:, 128:256])


def carry_kernel(sums_ref, out_ref, *start_refs):
    here = lax.axis_index("head")
    for d in range(4):
        group = lax.rem(here + d, 4)
        start_refs[d][...] = sums_ref[pl.ds(pl.multiple_of(group * 8, 8), 8), 40:72, :]
    carried = [jnp.zeros((8, 128), f32) for _ in range(4)]
    for m in reversed(range(sums_ref.shape[0])):
        for r in range(4):
            tile = slice(8 * r, 8 * r + 8)
            out_ref[m, tile, :] = carried[r]
            decay = jnp.broadcast_to(sums_ref[m, 32 + r : 33 + r, :], (8, 128))
            carried[r] = sums_ref[m, tile, :] + decay * carried[r]


def pair_kernel(
    x_ref, dy_ref, b_ref, c_ref, bt_ref, ct_ref, cols_ref, scales_ref, info_ref,
    adj_ref, rows_ref, into_ref, back_ref, gb_ref, gc_ref,
    tot_ref, meet_ref, scale_ref,
):
    g = pl.program_id(0)
    blocks = x_ref.shape[0] // Q

    @pl.when(g == 0)
    def clear():
        for k in range(blocks):
            rows = slice(k * Q, (k + 1) * Q)
            meet_ref[k] = dt(b_ref[rows, :], c_ref[rows, :])
        tot_ref[...] = jnp.zeros_like(tot_ref)

    skip = spread(group_cols(cols_ref[0:8, :], g), SKIP)[0:1, :]
    for source_ref, base, turn_ref, out_ref in (
        (x_ref, SHRINK, bt_ref, into_ref),
        (dy_ref, GROW, ct_ref, back_ref),
    ):
        scale_ref[...] = dn(scales_ref[...], repeater(base, g))
        for k in range(blocks):
            rows = slice(k * Q, (k + 1) * Q)
            high, low = split(source_ref[rows, :].astype(f32) * scale_ref[rows, :])
            turn = turn_ref[k]
            out_ref[0, k] = dn(side(turn, turn), stack(high, low))

    upper = lax.broadcasted_iota(jnp.int32, (Q, Q), 0) <= lax.broadcasted_iota(
        jnp.int32, (Q, Q), 1
    )
    lane = lax.broadcasted_iota(jnp.int32, (1, 128), 1)
    masks = [
        jnp.where(lane < 64, 1.0, 0.0).astype(bf16),
        jnp.where(lane < 64, 0.0, 1.0).astype(bf16),
    ]

    def one(k):
        rows = pl.ds(pl.multiple_of(k * Q, Q), Q)
        cols = group_cols(cols_ref[rows, :], g)
        meet = meet_ref[k]
        total = tot_ref[k]
        in_rows, products = [], []
        for j in range(2):
            lanes = slice(128 * j, 128 * j + 128)
            x_pair, dy_pair = x_ref[rows, lanes], dy_ref[rows, lanes]
            dots = dt(stack(x_pair * masks[0], x_pair * masks[1]), dy_pair)
            weights, values = [], []
            for i in range(2):
                h = 2 * j + i
                gap = info_ref[0, h : h + 1, rows] - jnp.broadcast_to(
                    cols[:, LOGCOL + h : LOGCOL + h + 1], (Q, Q)
                )
                decay = jnp.exp2(jnp.where(upper, gap, -1e30))
                pair = dots[Q * i : Q * i + Q] * decay
                total = total + pair
                in_rows.append(jnp.sum(pair * meet, axis=0, keepdims=True))
                weights += list(split(decay * meet))
                values += [dy_pair * masks[i]] * 2
            adj = dn(side(*weights), stack(*values))
            adj_ref[0, rows, lanes] = adj + skip[:, lanes] * dy_pair.astype(f32)
            products.append(x_pair.astype(f32) * adj)
        tot_ref[k] = total
        rows_ref[0, 0:4, rows] = stack(*in_rows)
        rows_ref[0, 4:8, rows] = head_sums(side(*products))

    def some(i, unused):
        for k in range(PAIR_UNROLL):
            one(i * PAIR_UNROLL + k)
        return unused

    lax.fori_loop(0, blocks // PAIR_UNROLL, some, 0)

    @pl.when(g == pl.num_programs(0) - 1)
    def finish():
        for k in range(blocks):
            rows = slice(k * Q, (k + 1) * Q)
            total = tot_ref[k]
            high, low = split(total)
            c = c_ref[rows, :]
            gb_ref[rows, :] = dn(side(high, low), stack(c, c))
            high, low = split(total.T)
            b = b_ref[rows, :]
            gc_ref[rows, :] = dn(side(high, low), stack(b, b))


PAIR_UNROLL = 8


def three(rows_high, rows_low, high, low):
    both = dt(rows_high, stack(high, low))
    return both[:, 0:128] + both[:, 128:256] + dt(rows_low, high)


def forward_kernel(
    dy_ref, c_ref, into_ref, scales_ref, start0_ref, start1_ref, start2_ref, start3_ref, gc_in_ref,
    gc_ref, rows_ref, end_ref,
    hold_ref, grow_ref,
):
    g = pl.program_id(0)
    blocks = dy_ref.shape[0] // Q

    @pl.when(g == 0)
    def copy():
        gc_ref[...] = gc_in_ref[...]

    here = lax.axis_index("head")
    for d, start_ref in enumerate((start0_ref, start1_ref, start2_ref, start3_ref)):
        part = lax.rem(here + 4 - d, 4)
        for h in range(4):
            at = 16 * (h % 2)
            to = pl.ds(pl.multiple_of(64 * h + 16 * part, 16), 16)
            hold_ref[to, :] = start_ref[h // 2, at : at + 16, :]
    state = hold_ref[...].T
    grow_ref[...] = dn(scales_ref[...], repeater(GROW, g))
    for k in range(blocks):
        rows = slice(k * Q, (k + 1) * Q)
        grow = grow_ref[rows, :]
        s_high, s_low = split(state)
        c = c_ref[rows, :]
        from_state = dn(side(c, c), stack(s_high, s_low))
        dy_grown = dy_ref[rows, :].astype(f32) * grow
        dy_high, dy_low = split(dy_grown)
        rows_ref[0, 0:4, rows] = head_sums(dy_grown * from_state)
        gc_ref[rows, :] += three(dy_high, dy_low, s_high, s_low)
        state = grow[Q - 1 : Q, :] * state + into_ref[0, k]
    end_ref[0] = state


def backward_kernel(
    x_ref, b_ref, scales_ref, info_ref, back_ref, adj_ref, gb_in_ref,
    pair_rows_ref, rows_ref, end_ref, in_ref,
    gx_ref, raw_ref, gb0_ref, gb1_ref, gb2_ref, gb3_ref,
    gb_ref, keep_ref, through_ref, shrink_ref,
):
    g = pl.program_id(0)
    blocks = x_ref.shape[0] // Q

    @pl.when(g == 0)
    def copy():
        gb_ref[...] = gb_in_ref[...]

    adjoint = side(*[in_ref[:, 0, 8 * r : 8 * r + 8, :].reshape(128, 128) for r in range(2)])
    meeting = jnp.sum(adjoint * end_ref[0], axis=0, keepdims=True)
    row = lax.broadcasted_iota(jnp.int32, (8, 256), 0)
    lane = lax.broadcasted_iota(jnp.int32, (8, 256), 1)
    through = jnp.sum(jnp.where(row == lane // 64, meeting, 0.0), axis=1, keepdims=True)[0:4]
    shrink_ref[...] = dn(scales_ref[...], repeater(SHRINK, g))
    ends = stack(*[scales_ref[k * Q + Q - 16 : k * Q + Q, :] for k in range(blocks)])
    decays = dn(ends, repeater(GROW, g))
    for k in reversed(range(blocks)):
        rows = slice(k * Q, (k + 1) * Q)
        shrink = shrink_ref[rows, :]
        x_full = x_ref[rows, :].astype(f32)
        x_high, x_low = split(x_full * shrink)
        g_high, g_low = split(adjoint)
        b = b_ref[rows, :]
        adj = shrink * dn(side(b, b), stack(g_high, g_low))
        gx_ref[rows, :] = (adj_ref[0, rows, :] + adj).astype(bf16)
        out_rows = pair_rows_ref[0, 4:8, rows] + head_sums(x_full * adj)
        gb_ref[rows, :] += three(x_high, x_low, g_high, g_low)
        adjoint = decays[16 * k + 15 : 16 * k + 16, :] * adjoint + back_ref[0, k]
        keep_ref[g, 0:4, rows] = (
            pair_rows_ref[0, 0:4, rows] + rows_ref[0, 0:4, rows] - out_rows
        )
        keep_ref[g, 4:8, rows] = out_rows
    through_ref[g] = jnp.broadcast_to(through, (4, Q))

    @pl.when(g == pl.num_programs(0) - 1)
    def finish():
        here = lax.axis_index("head")
        for d, part_ref in enumerate((gb0_ref, gb1_ref, gb2_ref, gb3_ref)):
            size = part_ref.shape[0]
            at = lax.rem(here + d, 4) * size
            part_ref[...] = gb_ref[pl.ds(pl.multiple_of(at, size), size), :]
        after = jnp.where(
            lax.broadcasted_iota(jnp.int32, (Q, Q), 0)
            >= lax.broadcasted_iota(jnp.int32, (Q, Q), 1),
            1.0, 0.0,
        )

        def all_heads(ref, first, rows):
            return stack(*[ref[r, first : first + 4, rows] for r in range(4)])

        parts = [all_heads(keep_ref, 0, slice(k * Q, (k + 1) * Q)) for k in range(blocks)]
        sums = dn(stack(*parts), after, HIGHEST)
        later = stack(*[through_ref[r][:, 0:1] for r in range(4)])
        for k in reversed(range(blocks)):
            rows = slice(k * Q, (k + 1) * Q)
            here = sums[16 * k : 16 * k + 16]
            step, gate, rate = (all_heads(info_ref, 4 * r, rows) for r in (1, 2, 3))
            x_adj = all_heads(keep_ref, 4, rows)
            raw_ref[:, rows] = gate * (x_adj / step - rate * (here + later))
            later = later + here[:, 0:1]


def whole(shape):
    zeros = (0,) * len(shape)
    return pl.BlockSpec(tuple(shape), lambda g, zeros=zeros: zeros)


def around(array, distance):
    if distance == 0:
        return array
    heads = lax.axis_size("head")
    return lax.ppermute(array, "head", [(i, (i + distance) % heads) for i in range(heads)])


def on_device(
    inputs, out_grad, b_proj, c_proj, step_raw, log_rate, step_bias, skip_gain,
    saved_states, segment_slot,
):
    tok = inputs.shape[0]
    blocks = tok // Q
    segs = saved_states.shape[0]
    arbitrary = pltpu.CompilerParams(dimension_semantics=("arbitrary",))

    def shape(*dims, dtype=f32):
        return jax.ShapeDtypeStruct(dims, dtype)

    def cost(flops, bytes_accessed):
        return pl.CostEstimate(
            flops=flops, transcendentals=0, bytes_accessed=bytes_accessed
        )

    quarter = pl.BlockSpec((tok, 256), lambda g: (0, g))
    narrow = whole((tok, 128))
    rows8 = pl.BlockSpec((1, 8, tok), lambda g: (g, 0, 0))
    info_spec = pl.BlockSpec((1, 16, tok), lambda g: (g, 0, 0))
    turn = whole((blocks, 128, Q))
    states = pl.BlockSpec((1, blocks, 128, 256), lambda g: (g, 0, 0, 0))
    block = pl.BlockSpec((1, tok, 256), lambda g: (g, 0, 0))
    state = pl.BlockSpec((1, 128, 256), lambda g: (g, 0, 0))
    sums, cols, scales, info, bt, ct = pl.pallas_call(
        first_kernel,
        grid=(4,),
        in_specs=[
            pl.BlockSpec(memory_space=pltpu.SMEM), whole((16, tok)), whole((1, 16)),
            whole((1, 16)), whole((1, 16)), quarter,
            narrow, narrow, whole((segs, 32, 128)),
        ],
        out_specs=[
            whole((segs, 72, 128)), narrow, narrow, whole((4, 16, tok)), turn, turn,
        ],
        out_shape=(
            shape(segs, 72, 128), shape(tok, 128), shape(tok, 128, dtype=bf16),
            shape(4, 16, tok), shape(blocks, 128, Q, dtype=bf16),
            shape(blocks, 128, Q, dtype=bf16),
        ),
        scratch_shapes=[pltpu.VMEM((128, 128), f32)],
        compiler_params=arbitrary,
        cost_estimate=cost(10**9, 10**7),
        name="first",
    )(
        segment_slot, step_raw.T, log_rate[None], step_bias[None], skip_gain[None], out_grad, b_proj, c_proj,
        saved_states.reshape(segs, 32, 128),
    )
    sums = lax.all_to_all(sums, "seq", split_axis=0, concat_axis=0, tiled=True)

    adj, pair_rows, into, back, gb, gc = pl.pallas_call(
        pair_kernel,
        grid=(4,),
        in_specs=[
            quarter, quarter, narrow, narrow, turn, turn, narrow, narrow, info_spec
        ],
        out_specs=[block, rows8, states, states, narrow, narrow],
        out_shape=[
            shape(4, tok, 256), shape(4, 8, tok), shape(4, blocks, 128, 256),
            shape(4, blocks, 128, 256), shape(tok, 128), shape(tok, 128),
        ],
        scratch_shapes=[
            pltpu.VMEM((blocks, Q, Q), f32), pltpu.VMEM((blocks, Q, Q), f32),
            pltpu.VMEM((tok, 256), f32),
        ],
        compiler_params=arbitrary,
        cost_estimate=cost(2 * 10**10, 10**7),
        name="pairs",
    )(inputs, out_grad, b_proj, c_proj, bt, ct, cols, scales, info)
    sums, gb = lax.optimization_barrier((sums, gb))
    carried, *starts = pl.pallas_call(
        carry_kernel,
        grid=(1,),
        in_specs=[whole((segs, 72, 128))],
        out_specs=[whole((segs, 32, 128))] + [whole((8, 32, 128))] * 4,
        out_shape=[shape(segs, 32, 128)] + [shape(8, 32, 128)] * 4,
        compiler_params=pltpu.CompilerParams(vmem_limit_bytes=8 * 2**20),
        cost_estimate=cost(10**6, 10**6),
        name="carry",
    )(sums)
    shifted = []
    for d, start in enumerate(starts):
        shifted.append(around(start, d))
    incoming = lax.all_to_all(carried, "seq", split_axis=0, concat_axis=0, tiled=True)
    gc, rows, end = pl.pallas_call(
        forward_kernel,
        grid=(4,),
        in_specs=[
            quarter, narrow, states, narrow,
            *[pl.BlockSpec((2, 32, 128), lambda g: (g, 0, 0))] * 4, narrow,
        ],
        out_specs=[narrow, rows8, state],
        out_shape=(
            shape(tok, 128), shape(4, 8, tok), shape(4, 128, 256),
        ),
        scratch_shapes=[
            pltpu.VMEM((256, 128), f32), pltpu.VMEM((tok, 256), f32)
        ],
        compiler_params=arbitrary,
        cost_estimate=cost(3 * 10**9, 10**7),
        name="forward",
    )(out_grad, c_proj, into, scales, *shifted, gc)
    gc = lax.all_to_all(
        gc.reshape(4, tok // 4, 128), "head", split_axis=0, concat_axis=0, tiled=True
    ).sum(axis=0)
    grad_inputs, grad_step_raw, *gbs = pl.pallas_call(
        backward_kernel,
        grid=(4,),
        in_specs=[
            quarter, narrow, narrow, whole((4, 16, tok)), states,
            block, narrow, rows8,
            rows8, state,
            pl.BlockSpec((16, 1, 16, 128), lambda g: (0, g // 2, g % 2, 0)),
        ],
        out_specs=[quarter, whole((16, tok))] + [whole((tok // 4, 128))] * 4,
        out_shape=[shape(tok, 1024, dtype=bf16), shape(16, tok)] + [shape(tok // 4, 128)] * 4,
        scratch_shapes=[
            pltpu.VMEM((tok, 128), f32), pltpu.VMEM((4, 8, tok), f32), pltpu.VMEM((4, 4, Q), f32), pltpu.VMEM((tok, 256), f32)
        ],
        compiler_params=arbitrary,
        cost_estimate=cost(3 * 10**9, 10**7),
        name="backward",
    )(
        inputs, b_proj, scales, info, back, adj, gb, pair_rows, rows,
        end, incoming.reshape(16, 2, 32, 128),
    )
    far = around(gbs[2], 2)
    gb = gbs[0] + around(gbs[1], 1) + around(gbs[3], 3) + far
    return grad_inputs, grad_step_raw.T, gb, gc


def solution(mesh):
    return jax.shard_map(
        on_device,
        mesh=mesh,
        in_specs=(
            P("seq", "head"),
            P("seq", "head"),
            P("seq", None),
            P("seq", None),
            P("seq", "head"),
            P("head"),
            P("head"),
            P("head"),
            P(None, "seq", "head", None),
            P(),
        ),
        out_specs=(P("seq", "head"), P("seq", "head"), P(("seq", "head"), None), P(("seq", "head"), None)),
        check_vma=False,
    )
```

profile of v0, /device:TPU:1, one launch (start us, length us, event | category | flops | bytes accessed | tf_op | source)
XLA Modules:
  0.0 83.5 jit_solution(16407340377902964062)
XLA Ops:
  0.6 7.1 %first.1 = (f32[32,72,128]{2,1,0:T(8,128)}, f32[1024,128]{1,0:T(8,128)}, bf16[1024,128]{1,0:T(8,128)(2,1)}, f32[4,16,1024]{2,1,0:T(8,128)}, bf16[8,128,128]{2,1,0:T(8,128)(2,1)}, /*index=5*/bf16[8,128,128]{2,1,0:T(8,128)(2,1)}) custom-call(s32[32]{0:T(128)} %slot_ref.1, f32[16,1024]{1,0:T(8,128)} %bitcast.11, f32[1,16]{1,0:T(1,128)} %bitcast.13, ...), custom_call_target="tpu_custom_call" | custom-call | flops 1000000000 | bytes 10000000 | tf_op jit(solution)/shard_map/first/pallas_call | solution.py:414
  7.7 9.4 %all-to-all-start = ((f32[32,72,128]{2,1,0:T(8,128)}), f32[32,72,128]{2,1,0:T(8,128)S(1)}, u32[]{:S(2)}, u32[]{:S(2)}) async-start(f32[32,72,128]{2,1,0:T(8,128)} %get-tuple-element.39), calls=%async_computation | async-start | bytes 2359296 | tf_op jit(solution)/shard_map/all_to_all | solution.py:438
  17.2 14.1 %pairs.1 = (f32[4,1024,256]{2,1,0:T(8,128)}, f32[4,8,1024]{2,1,0:T(8,128)}, f32[4,8,128,256]{3,2,1,0:T(8,128)}, f32[4,8,128,256]{3,2,1,0:T(8,128)}, f32[1024,128]{1,0:T(8,128)}, /*index=5*/f32[1024,128]{1,0:T(8,128)}) custom-call(bf16[1024,1024]{1,0:T(8,128)(2,1)} %x_ref.3, bf16[1024,1024]{1,0:T(8,128)(2,1)} %dy_ref.5, bf16[1024,128]{1,0:T(8,128)(2,1)} %b_ref.5, ...), custom_call_target="tpu_custom_call" | custom-call | flops 20000000000 | bytes 10000000 | tf_op jit(solution)/shard_map/pairs/pallas_call | solution.py:440
  31.3 4.3 %all-to-all-done.sums_ref = f32[32,72,128]{2,1,0:T(8,128)S(1)} async-done(((f32[32,72,128]{2,1,0:T(8,128)}), f32[32,72,128]{2,1,0:T(8,128)S(1)}, u32[]{:S(2)}, u32[]{:S(2)}) %all-to-all-start) | async-done | bytes 1179680 | tf_op jit(solution)/shard_map/all_to_all | solution.py:438
  35.5 0.9 %carry.1 = (f32[32,32,128]{2,1,0:T(8,128)}, f32[8,32,128]{2,1,0:T(8,128)S(1)}, f32[8,32,128]{2,1,0:T(8,128)S(1)}, f32[8,32,128]{2,1,0:T(8,128)S(1)}, f32[8,32,128]{2,1,0:T(8,128)S(1)}) custom-call(f32[32,72,128]{2,1,0:T(8,128)S(1)} %all-to-all-done.sums_ref), custom_call_target="tpu_custom_call" | custom-call | flops 1000000 | bytes 1000000 | tf_op jit(solution)/shard_map/carry/pallas_call | solution.py:460
  36.4 0.7 copy-done
  37.0 3.9 %all-to-all-start.1 = ((f32[32,32,128]{2,1,0:T(8,128)}), f32[32,32,128]{2,1,0:T(8,128)S(1)}, u32[]{:S(2)}, u32[]{:S(2)}) async-start(f32[32,32,128]{2,1,0:T(8,128)} %get-tuple-element.52), calls=%async_computation.1 | async-start | bytes 1048576 | tf_op jit(solution)/shard_map/all_to_all | solution.py:473
  40.9 1.4 %collective-permute-start = (f32[8,32,128]{2,1,0:T(8,128)S(1)}, f32[8,32,128]{2,1,0:T(8,128)S(1)}, u32[]{:S(2)}, u32[]{:S(2)}) collective-permute-start(f32[8,32,128]{2,1,0:T(8,128)S(1)} %get-tuple-element.46), channel_id=1, source_target_pairs={{0,1},{1,2},{2,3},{3,0},{4,5},{5,6},{6,7},{7,4},{8,9},{9,10},{10,1... | collective-permute-start | bytes 393224 | tf_op jit(solution)/shard_map/ppermute | solution.py:386
  42.3 2.6 %collective-permute-start.1 = (f32[8,32,128]{2,1,0:T(8,128)S(1)}, f32[8,32,128]{2,1,0:T(8,128)S(1)}, u32[]{:S(2)}, u32[]{:S(2)}) collective-permute-start(f32[8,32,128]{2,1,0:T(8,128)S(1)} %get-tuple-element.47), channel_id=1, source_target_pairs={{0,2},{1,3},{2,0},{3,1},{4,6},{5,7},{6,4},{7,5},{8,10},{9,11},{10,... | collective-permute-start | bytes 393224 | tf_op jit(solution)/shard_map/ppermute | solution.py:386
  44.9 1.1 %collective-permute-start.2 = (f32[8,32,128]{2,1,0:T(8,128)S(1)}, f32[8,32,128]{2,1,0:T(8,128)S(1)}, u32[]{:S(2)}, u32[]{:S(2)}) collective-permute-start(f32[8,32,128]{2,1,0:T(8,128)S(1)} %get-tuple-element.48), channel_id=1, source_target_pairs={{0,3},{1,0},{2,1},{3,2},{4,7},{5,4},{6,5},{7,6},{8,11},{9,8},{10,9... | collective-permute-start | bytes 393224 | tf_op jit(solution)/shard_map/ppermute | solution.py:386
  46.0 1.2 %collective-permute-done.start1_ref = f32[8,32,128]{2,1,0:T(8,128)S(1)} collective-permute-done((f32[8,32,128]{2,1,0:T(8,128)S(1)}, f32[8,32,128]{2,1,0:T(8,128)S(1)}, u32[]{:S(2)}, u32[]{:S(2)}) %collective-permute-start) | collective-permute-done | bytes 131104 | tf_op jit(solution)/shard_map/ppermute | solution.py:386
  47.2 3.9 %collective-permute-done.1.start2_ref = f32[8,32,128]{2,1,0:T(8,128)S(1)} collective-permute-done((f32[8,32,128]{2,1,0:T(8,128)S(1)}, f32[8,32,128]{2,1,0:T(8,128)S(1)}, u32[]{:S(2)}, u32[]{:S(2)}) %collective-permute-start.1) | collective-permute-done | bytes 131104 | tf_op jit(solution)/shard_map/ppermute | solution.py:386
  51.1 0.6 copy-done.3
  51.8 7.6 %forward.1 = (f32[1024,128]{1,0:T(8,128)}, f32[4,8,1024]{2,1,0:T(8,128)}, f32[4,128,256]{2,1,0:T(8,128)}) custom-call(bf16[1024,1024]{1,0:T(8,128)(2,1)} %dy_ref.5, bf16[1024,128]{1,0:T(8,128)(2,1)} %c_ref.5, f32[4,8,128,256]{3,2,1,0:T(8,128)} %get-tuple-element.43.into_ref, bf16[1024,128]{1,0:T(8,128)(2,1)} %get-tuple-element.32.scales_ref, ...), custom_call_target="tpu_custom_call" | custom-call | flops 3000000000 | bytes 10000000 | tf_op jit(solution)/shard_map/forward/pallas_call | solution.py:474
  59.4 3.5 %all-to-all-start.2 = ((f32[4,256,128]{2,1,0:T(8,128)}), f32[4,256,128]{2,1,0:T(8,128)S(1)}, u32[]{:S(2)}, u32[]{:S(2)}) async-start(f32[4,256,128]{2,1,0:T(8,128)} %bitcast.9), calls=%async_computation.2 | async-start | bytes 1048576 | tf_op jit(solution)/shard_map/all_to_all | solution.py:492
  62.9 9.6 %backward.1 = (bf16[1024,1024]{1,0:T(8,128)(2,1)}, f32[16,1024]{1,0:T(8,128)}, f32[256,128]{1,0:T(8,128)}, f32[256,128]{1,0:T(8,128)}, f32[256,128]{1,0:T(8,128)}, /*index=5*/f32[256,128]{1,0:T(8,128)}) custom-call(bf16[1024,1024]{1,0:T(8,128)(2,1)} %x_ref.3, bf16[1024,128]{1,0:T(8,128)(2,1)} %b_ref.5, bf16[1024,128]{1,0:T(8,128)(2,1)} %get-tuple-element.32.scales_ref, ...), custom_call_target="tpu_custom_call" | custom-call | flops 3000000000 | bytes 10000000 | tf_op jit(solution)/shard_map/backward/pallas_call | solution.py:495
  72.5 1.5 %collective-permute-start.3 = (f32[256,128]{1,0:T(8,128)}, f32[256,128]{1,0:T(8,128)S(1)}, u32[]{:S(2)}, u32[]{:S(2)}) collective-permute-start(f32[256,128]{1,0:T(8,128)} %get-tuple-element.56), channel_id=1, source_target_pairs={{0,1},{1,2},{2,3},{3,0},{4,5},{5,6},{6,7},{7,4},{8,9},{9,10},{10,1... | collective-permute-start | bytes 393224 | tf_op jit(solution)/shard_map/ppermute | solution.py:386
  74.0 1.3 %collective-permute-start.4 = (f32[256,128]{1,0:T(8,128)}, f32[256,128]{1,0:T(8,128)S(1)}, u32[]{:S(2)}, u32[]{:S(2)}) collective-permute-start(f32[256,128]{1,0:T(8,128)} %get-tuple-element.57), channel_id=1, source_target_pairs={{0,3},{1,0},{2,1},{3,2},{4,7},{5,4},{6,5},{7,6},{8,11},{9,8},{10,9... | collective-permute-start | bytes 393224 | tf_op jit(solution)/shard_map/ppermute | solution.py:386
  75.3 1.7 %collective-permute-start.5 = (f32[256,128]{1,0:T(8,128)}, f32[256,128]{1,0:T(8,128)S(1)}, u32[]{:S(2)}, u32[]{:S(2)}) collective-permute-start(f32[256,128]{1,0:T(8,128)} %get-tuple-element.58), channel_id=1, source_target_pairs={{0,2},{1,3},{2,0},{3,1},{4,6},{5,7},{6,4},{7,5},{8,10},{9,11},{10,... | collective-permute-start | bytes 393224 | tf_op jit(solution)/shard_map/ppermute | solution.py:386
  76.9 0.7 reduce_sum.9
  77.6 0.2 collective-permute-done.3
  77.8 0.2 collective-permute-done.4
  78.0 3.9 %collective-permute-done.5 = f32[256,128]{1,0:T(8,128)S(1)} collective-permute-done((f32[256,128]{1,0:T(8,128)}, f32[256,128]{1,0:T(8,128)S(1)}, u32[]{:S(2)}, u32[]{:S(2)}) %collective-permute-start.5) | collective-permute-done | bytes 131104 | tf_op jit(solution)/shard_map/ppermute | solution.py:386
  81.9 1.6 %add_add_fusion = f32[256,128]{1,0:T(8,128)} fusion(f32[256,128]{1,0:T(8,128)S(1)} %collective-permute-done.5, f32[256,128]{1,0:T(8,128)S(1)} %collective-permute-done.4, f32[256,128]{1,0:T(8,128)} %get-tuple-element.55, f32[256,128]{1,0:T(8,128)S(1)} %collective-permute-done.3), kind=kLoop, calls=%fused_computation | loop fusion | flops 98304 | bytes 655360 | tf_op jit(solution)/shard_map/add | solution.py:517
  (11 shorter events, 0.1 us)
Async XLA Ops:
  7.7 27.8 %all-to-all-start = ((f32[32,72,128]{2,1,0:T(8,128)}), f32[32,72,128]{2,1,0:T(8,128)S(1)}, u32[]{:S(2)}, u32[]{:S(2)}) async-start(f32[32,72,128]{2,1,0:T(8,128)} %get-tuple-element.39), calls=%async_computation | async-start | bytes 2359296 | tf_op jit(solution)/shard_map/all_to_all | solution.py:438
  36.4 0.7 copy-start
  37.0 22.4 %all-to-all-start.1 = ((f32[32,32,128]{2,1,0:T(8,128)}), f32[32,32,128]{2,1,0:T(8,128)S(1)}, u32[]{:S(2)}, u32[]{:S(2)}) async-start(f32[32,32,128]{2,1,0:T(8,128)} %get-tuple-element.52), calls=%async_computation.1 | async-start | bytes 1048576 | tf_op jit(solution)/shard_map/all_to_all | solution.py:473
  40.9 6.2 %collective-permute-start = (f32[8,32,128]{2,1,0:T(8,128)S(1)}, f32[8,32,128]{2,1,0:T(8,128)S(1)}, u32[]{:S(2)}, u32[]{:S(2)}) collective-permute-start(f32[8,32,128]{2,1,0:T(8,128)S(1)} %get-tuple-element.46), channel_id=1, source_target_pairs={{0,1},{1,2},{2,3},{3,0},{4,5},{5,6},{6,7},{7,4},{8,9},{9,10},{10,1... | collective-permute-start | bytes 393224 | tf_op jit(solution)/shard_map/ppermute | solution.py:386
  42.3 8.8 %collective-permute-start.1 = (f32[8,32,128]{2,1,0:T(8,128)S(1)}, f32[8,32,128]{2,1,0:T(8,128)S(1)}, u32[]{:S(2)}, u32[]{:S(2)}) collective-permute-start(f32[8,32,128]{2,1,0:T(8,128)S(1)} %get-tuple-element.47), channel_id=1, source_target_pairs={{0,2},{1,3},{2,0},{3,1},{4,6},{5,7},{6,4},{7,5},{8,10},{9,11},{10,... | collective-permute-start | bytes 393224 | tf_op jit(solution)/shard_map/ppermute | solution.py:386
  44.9 6.2 %collective-permute-start.2 = (f32[8,32,128]{2,1,0:T(8,128)S(1)}, f32[8,32,128]{2,1,0:T(8,128)S(1)}, u32[]{:S(2)}, u32[]{:S(2)}) collective-permute-start(f32[8,32,128]{2,1,0:T(8,128)S(1)} %get-tuple-element.48), channel_id=1, source_target_pairs={{0,3},{1,0},{2,1},{3,2},{4,7},{5,4},{6,5},{7,6},{8,11},{9,8},{10,9... | collective-permute-start | bytes 393224 | tf_op jit(solution)/shard_map/ppermute | solution.py:386
  47.2 3.9 %copy-start.2 = (f32[8,32,128]{2,1,0:T(8,128)}, f32[8,32,128]{2,1,0:T(8,128)S(1)}, u32[]{:S(2)}) copy-start(f32[8,32,128]{2,1,0:T(8,128)S(1)} %collective-permute-done.start1_ref) | copy-start | bytes 393220
  51.1 0.6 copy-start.3
  51.1 0.7 copy-start.4
  59.4 3.5 %copy-start.1 = (f32[32,32,128]{2,1,0:T(8,128)}, f32[32,32,128]{2,1,0:T(8,128)S(1)}, u32[]{:S(2)}) copy-start(f32[32,32,128]{2,1,0:T(8,128)S(1)} %all-to-all-done.1) | copy-start | bytes 1572868
  59.4 17.5 %all-to-all-start.2 = ((f32[4,256,128]{2,1,0:T(8,128)}), f32[4,256,128]{2,1,0:T(8,128)S(1)}, u32[]{:S(2)}, u32[]{:S(2)}) async-start(f32[4,256,128]{2,1,0:T(8,128)} %bitcast.9), calls=%async_computation.2 | async-start | bytes 1048576 | tf_op jit(solution)/shard_map/all_to_all | solution.py:492
  72.5 5.3 %collective-permute-start.3 = (f32[256,128]{1,0:T(8,128)}, f32[256,128]{1,0:T(8,128)S(1)}, u32[]{:S(2)}, u32[]{:S(2)}) collective-permute-start(f32[256,128]{1,0:T(8,128)} %get-tuple-element.56), channel_id=1, source_target_pairs={{0,1},{1,2},{2,3},{3,0},{4,5},{5,6},{6,7},{7,4},{8,9},{9,10},{10,1... | collective-permute-start | bytes 393224 | tf_op jit(solution)/shard_map/ppermute | solution.py:386
  74.0 4.0 %collective-permute-start.4 = (f32[256,128]{1,0:T(8,128)}, f32[256,128]{1,0:T(8,128)S(1)}, u32[]{:S(2)}, u32[]{:S(2)}) collective-permute-start(f32[256,128]{1,0:T(8,128)} %get-tuple-element.57), channel_id=1, source_target_pairs={{0,3},{1,0},{2,1},{3,2},{4,7},{5,4},{6,5},{7,6},{8,11},{9,8},{10,9... | collective-permute-start | bytes 393224 | tf_op jit(solution)/shard_map/ppermute | solution.py:386
  75.3 6.6 %collective-permute-start.5 = (f32[256,128]{1,0:T(8,128)}, f32[256,128]{1,0:T(8,128)S(1)}, u32[]{:S(2)}, u32[]{:S(2)}) collective-permute-start(f32[256,128]{1,0:T(8,128)} %get-tuple-element.58), channel_id=1, source_target_pairs={{0,2},{1,3},{2,0},{3,1},{4,6},{5,7},{6,4},{7,5},{8,10},{9,11},{10,... | collective-permute-start | bytes 393224 | tf_op jit(solution)/shard_map/ppermute | solution.py:386
where the time goes:
time: 85.1 us; the launch traced here: 83.5 us
  Pallas kernels  39.2 us (46%)
  starting transfers between devices  26.3 us (31%)
  waiting for transfers between devices  13.6 us (16%)
  other arithmetic  2.27 us (3%)
  local copies, waits for them, and re-layouts  1.36 us (2%)
    pallas_call x1, Pallas kernels, on_device(): pl.pallas_call(pair_kernel, grid=(4,), in_specs=[quarter, quarter, narrow...  14.1 us
    pallas_call x1, Pallas kernels, on_device(): pl.pallas_call(backward_kernel, grid=(4,), in_specs=[quarter, narrow, nar...  9.55 us
    ppermute x6, starting transfers between devices, around(): lax.ppermute(array, 'head', [(i, (i + distance) % heads) for i in range(h...  9.49 us
    all_to_all x1, starting transfers between devices, on_device(): sums = lax.all_to_all(sums, 'seq', split_axis=0, concat_axis=0, tiled=True)  9.43 us
    ppermute x6, waiting for transfers between devices, around(): lax.ppermute(array, 'head', [(i, (i + distance) % heads) for i in range(h...  9.37 us
    pallas_call x1, Pallas kernels, on_device(): pl.pallas_call(forward_kernel, grid=(4,), in_specs=[quarter, narrow, stat...  7.64 us
    pallas_call x1, Pallas kernels, on_device(): pl.pallas_call(first_kernel, grid=(4,), in_specs=[pl.BlockSpec(memory_spa...  7.09 us
    all_to_all x1, waiting for transfers between devices, on_device(): sums = lax.all_to_all(sums, 'seq', split_axis=0, concat_axis=0, tiled=True)  4.25 us
  transfers between devices with their start and end apart: 9, of which 6 were waited for; matrix products, arithmetic and copies ran while one was open for 1% of the time, Pallas kernels for 37%

commit v1 on v0

--- a/solution.py
+++ b/solution.py
@@ -68,8 +68,8 @@
     return stack(*rows)
 
 
-GROW, SHRINK = 0, 32
-LOGCOL, GROW_ALL, SKIP = (16 * q for q in range(3))
+GROW, SHRINK, GROW_ALL = 0, 32, 64
+LOGCOL, SKIP = 0, 16
 
 
 def repeater(base, group):
@@ -79,9 +79,9 @@
 
 
 def first_kernel(
-    slot_ref, raw_ref, rate_ref, bias_ref, skip_ref, dy_ref, b_ref, c_ref, saved_ref,
-    sums_ref, cols_ref, scales_ref, info_ref, bt_ref, ct_ref,
-    pad_ref,
+    slot_ref, raw_ref, rate_ref, bias_ref, skip_ref, dy_ref, c_ref, saved_ref,
+    sums_ref, scales_ref, info_ref,
+    pad_ref, ct_ref,
 ):
     g = pl.program_id(0)
     blocks = dy_ref.shape[0] // Q
@@ -112,38 +112,29 @@
         logs = [sums[16 * k : 16 * k + 16] for k in range(blocks)]
         ends = [log[:, Q - 1 : Q] for log in logs]
         so_far = jnp.zeros_like(ends[0])
-        fill = jnp.zeros((80, Q), f32)
-        fill_scales = jnp.zeros((64, Q), f32)
+        fill = jnp.zeros((32, Q), f32)
         for k in range(blocks):
             log, step = logs[k], steps[k]
-            cols_ref[k * Q : (k + 1) * Q, :] = stack(
-                log - jnp.log(step) * LOG2E,
-                jnp.exp2(log + so_far),
-                skip,
-                fill,
-            ).T
-            grow, shrink = jnp.exp2(log), step * jnp.exp2(ends[k] - log)
-            grow_high, shrink_high = (
-                part.astype(bf16).astype(f32) for part in (grow, shrink)
-            )
-            scales_ref[k * Q : (k + 1) * Q, :] = stack(
-                grow_high, grow - grow_high, shrink_high, shrink - shrink_high, fill_scales
-            ).T.astype(bf16)
+            parts = []
+            for part in (
+                jnp.exp2(log), step * jnp.exp2(ends[k] - log), jnp.exp2(log + so_far)
+            ):
+                high = part.astype(bf16).astype(f32)
+                parts += [high, part - high]
+            scales_ref[k * Q : (k + 1) * Q, :] = stack(*parts, fill).T.astype(bf16)
             so_far = so_far + ends[k]
             for r in range(4):
                 four = slice(4 * r, 4 * r + 4)
                 info_ref[r, :, k * Q : (k + 1) * Q] = stack(
-                    log[four], step[four], gates[k][four], rate[four]
+                    log[four], step[four], gates[k][four], rate[four], skip[four], skip[four]
                 )
             ct_ref[k] = c_ref[k * Q : (k + 1) * Q, :].astype(f32).T.astype(bf16)
-            bt_ref[k] = b_ref[k * Q : (k + 1) * Q, :].astype(f32).T.astype(bf16)
-        zero_rows = jnp.zeros((4, 128), f32)
         ends_row = []
         for r in range(4):
-            last = spread(cols_ref[blocks * Q - 8 : blocks * Q, :], GROW_ALL + 4 * r)[7:8, :]
-            ends_row += [last[:, 0:128], last[:, 128:256]]
+            last = dn(scales_ref[blocks * Q - 16 : blocks * Q, :], repeater(GROW_ALL, r))
+            ends_row += [last[15:16, 0:128], last[15:16, 128:256]]
         for half in range(2):
-            tile = stack(*ends_row[4 * half : 4 * half + 4], zero_rows)
+            tile = stack(*ends_row[4 * half : 4 * half + 4], jnp.zeros((4, 128), f32))
             for i in range(16):
                 sums_ref[2 * i + half, 32:40, :] = tile
 
@@ -180,9 +171,9 @@
 
 
 def pair_kernel(
-    x_ref, dy_ref, b_ref, c_ref, bt_ref, ct_ref, cols_ref, scales_ref, info_ref,
+    x_ref, dy_ref, b_ref, c_ref, scales_ref, info_ref,
     adj_ref, rows_ref, into_ref, back_ref, gb_ref, gc_ref,
-    tot_ref, meet_ref, scale_ref,
+    tot_ref, meet_ref, scale_ref, cols_ref, bt_ref, ct_ref,
 ):
     g = pl.program_id(0)
     blocks = x_ref.shape[0] // Q
@@ -192,6 +183,13 @@
         for k in range(blocks):
             rows = slice(k * Q, (k + 1) * Q)
             meet_ref[k] = dt(b_ref[rows, :], c_ref[rows, :])
+            ct_ref[k] = c_ref[rows, :].astype(f32).T.astype(bf16)
+            bt_ref[k] = b_ref[rows, :].astype(f32).T.astype(bf16)
+            logs = [
+                info_ref[r, 0:4, rows] - jnp.log(info_ref[r, 4:8, rows]) * LOG2E for r in range(4)
+            ]
+            skips = [info_ref[r, 16:20, rows] for r in range(4)]
+            cols_ref[rows, :] = stack(*logs, *skips, jnp.zeros((96, Q), f32)).T
         tot_ref[...] = jnp.zeros_like(tot_ref)
 
     skip = spread(group_cols(cols_ref[0:8, :], g), SKIP)[0:1, :]
@@ -228,7 +226,7 @@
             weights, values = [], []
             for i in range(2):
                 h = 2 * j + i
-                gap = info_ref[0, h : h + 1, rows] - jnp.broadcast_to(
+                gap = info_ref[g, h : h + 1, rows] - jnp.broadcast_to(
                     cols[:, LOGCOL + h : LOGCOL + h + 1], (Q, Q)
                 )
                 decay = jnp.exp2(jnp.where(upper, gap, -1e30))
@@ -308,10 +306,9 @@
 
 
 def backward_kernel(
-    x_ref, b_ref, scales_ref, info_ref, back_ref, adj_ref, gb_in_ref,
-    pair_rows_ref, rows_ref, end_ref, in_ref,
-    gx_ref, raw_ref, gb0_ref, gb1_ref, gb2_ref, gb3_ref,
-    gb_ref, keep_ref, through_ref, shrink_ref,
+    x_ref, scales_ref, back_ref, gb_in_ref, end_ref, in_ref,
+    through_ref, gb0_ref, gb1_ref, gb2_ref, gb3_ref,
+    gb_ref, shrink_ref,
 ):
     g = pl.program_id(0)
     blocks = x_ref.shape[0] // Q
@@ -324,27 +321,17 @@
     meeting = jnp.sum(adjoint * end_ref[0], axis=0, keepdims=True)
     row = lax.broadcasted_iota(jnp.int32, (8, 256), 0)
     lane = lax.broadcasted_iota(jnp.int32, (8, 256), 1)
-    through = jnp.sum(jnp.where(row == lane // 64, meeting, 0.0), axis=1, keepdims=True)[0:4]
+    through = jnp.sum(jnp.where(row == lane // 64, meeting, 0.0), axis=1, keepdims=True)
+    through_ref[0] = jnp.broadcast_to(through, (8, 128))
     shrink_ref[...] = dn(scales_ref[...], repeater(SHRINK, g))
     ends = stack(*[scales_ref[k * Q + Q - 16 : k * Q + Q, :] for k in range(blocks)])
     decays = dn(ends, repeater(GROW, g))
     for k in reversed(range(blocks)):
         rows = slice(k * Q, (k + 1) * Q)
-        shrink = shrink_ref[rows, :]
-        x_full = x_ref[rows, :].astype(f32)
-        x_high, x_low = split(x_full * shrink)
+        x_high, x_low = split(x_ref[rows, :].astype(f32) * shrink_ref[rows, :])
         g_high, g_low = split(adjoint)
-        b = b_ref[rows, :]
-        adj = shrink * dn(side(b, b), stack(g_high, g_low))
-        gx_ref[rows, :] = (adj_ref[0, rows, :] + adj).astype(bf16)
-        out_rows = pair_rows_ref[0, 4:8, rows] + head_sums(x_full * adj)
         gb_ref[rows, :] += three(x_high, x_low, g_high, g_low)
         adjoint = decays[16 * k + 15 : 16 * k + 16, :] * adjoint + back_ref[0, k]
-        keep_ref[g, 0:4, rows] = (
-            pair_rows_ref[0, 0:4, rows] + rows_ref[0, 0:4, rows] - out_rows
-        )
-        keep_ref[g, 4:8, rows] = out_rows
-    through_ref[g] = jnp.broadcast_to(through, (4, Q))
 
     @pl.when(g == pl.num_programs(0) - 1)
     def finish():
@@ -353,6 +340,34 @@
             size = part_ref.shape[0]
             at = lax.rem(here + d, 4) * size
             part_ref[...] = gb_ref[pl.ds(pl.multiple_of(at, size), size), :]
+
+
+def last_kernel(
+    x_ref, b_ref, scales_ref, info_ref, adj_ref, pair_rows_ref, rows_ref,
+    back_ref, in_ref, through_ref,
+    gx_ref, raw_ref,
+    keep_ref, shrink_ref,
+):
+    g = pl.program_id(0)
+    blocks = x_ref.shape[0] // Q
+    adjoint = side(*[in_ref[:, 0, 8 * r : 8 * r + 8, :].reshape(128, 128) for r in range(2)])
+    shrink_ref[...] = dn(scales_ref[...], repeater(SHRINK, g))
+    ends = stack(*[scales_ref[k * Q + Q - 16 : k * Q + Q, :] for k in range(blocks)])
+    decays = dn(ends, repeater(GROW, g))
+    for k in reversed(range(blocks)):
+        rows = slice(k * Q, (k + 1) * Q)
+        b = b_ref[rows, :]
+        adj = shrink_ref[rows, :] * dn(side(b, b), stack(*split(adjoint)))
+        adjoint = decays[16 * k + 15 : 16 * k + 16, :] * adjoint + back_ref[0, k]
+        gx_ref[rows, :] = (adj_ref[0, rows, :] + adj).astype(bf16)
+        out_rows = pair_rows_ref[0, 4:8, rows] + head_sums(x_ref[rows, :].astype(f32) * adj)
+        keep_ref[g, 0:4, rows] = (
+            pair_rows_ref[0, 0:4, rows] + rows_ref[0, 0:4, rows] - out_rows
+        )
+        keep_ref[g, 4:8, rows] = out_rows
+
+    @pl.when(g == pl.num_programs(0) - 1)
+    def finish():
         after = jnp.where(
             lax.broadcasted_iota(jnp.int32, (Q, Q), 0)
             >= lax.broadcasted_iota(jnp.int32, (Q, Q), 1),
@@ -364,7 +379,7 @@
 
         parts = [all_heads(keep_ref, 0, slice(k * Q, (k + 1) * Q)) for k in range(blocks)]
         sums = dn(stack(*parts), after, HIGHEST)
-        later = stack(*[through_ref[r][:, 0:1] for r in range(4)])
+        later = stack(*[through_ref[r, 0:4, 0:1] for r in range(4)])
         for k in reversed(range(blocks)):
             rows = slice(k * Q, (k + 1) * Q)
             here = sums[16 * k : 16 * k + 16]
@@ -406,34 +421,27 @@
     quarter = pl.BlockSpec((tok, 256), lambda g: (0, g))
     narrow = whole((tok, 128))
     rows8 = pl.BlockSpec((1, 8, tok), lambda g: (g, 0, 0))
-    info_spec = pl.BlockSpec((1, 16, tok), lambda g: (g, 0, 0))
-    turn = whole((blocks, 128, Q))
     states = pl.BlockSpec((1, blocks, 128, 256), lambda g: (g, 0, 0, 0))
     block = pl.BlockSpec((1, tok, 256), lambda g: (g, 0, 0))
     state = pl.BlockSpec((1, 128, 256), lambda g: (g, 0, 0))
-    sums, cols, scales, info, bt, ct = pl.pallas_call(
+    sums, scales, info = pl.pallas_call(
         first_kernel,
         grid=(4,),
         in_specs=[
             pl.BlockSpec(memory_space=pltpu.SMEM), whole((16, tok)), whole((1, 16)),
-            whole((1, 16)), whole((1, 16)), quarter,
-            narrow, narrow, whole((segs, 32, 128)),
-        ],
-        out_specs=[
-            whole((segs, 72, 128)), narrow, narrow, whole((4, 16, tok)), turn, turn,
-        ],
+            whole((1, 16)), whole((1, 16)), quarter, narrow, whole((segs, 32, 128)),
+        ],
+        out_specs=[whole((segs, 72, 128)), narrow, whole((4, 24, tok))],
         out_shape=(
-            shape(segs, 72, 128), shape(tok, 128), shape(tok, 128, dtype=bf16),
-            shape(4, 16, tok), shape(blocks, 128, Q, dtype=bf16),
-            shape(blocks, 128, Q, dtype=bf16),
+            shape(segs, 72, 128), shape(tok, 128, dtype=bf16), shape(4, 24, tok),
         ),
-        scratch_shapes=[pltpu.VMEM((128, 128), f32)],
+        scratch_shapes=[pltpu.VMEM((128, 128), f32), pltpu.VMEM((blocks, 128, Q), bf16)],
         compiler_params=arbitrary,
         cost_estimate=cost(10**9, 10**7),
         name="first",
     )(
-        segment_slot, step_raw.T, log_rate[None], step_bias[None], skip_gain[None], out_grad, b_proj, c_proj,
-        saved_states.reshape(segs, 32, 128),
+        segment_slot, step_raw.T, log_rate[None], step_bias[None], skip_gain[None], out_grad,
+        c_proj, saved_states.reshape(segs, 32, 128),
     )
     sums = lax.all_to_all(sums, "seq", split_axis=0, concat_axis=0, tiled=True)
 
@@ -441,7 +449,7 @@
         pair_kernel,
         grid=(4,),
         in_specs=[
-            quarter, quarter, narrow, narrow, turn, turn, narrow, narrow, info_spec
+            quarter, quarter, narrow, narrow, narrow, whole((4, 24, tok))
         ],
         out_specs=[block, rows8, states, states, narrow, narrow],
         out_shape=[
@@ -450,12 +458,13 @@
         ],
         scratch_shapes=[
             pltpu.VMEM((blocks, Q, Q), f32), pltpu.VMEM((blocks, Q, Q), f32),
-            pltpu.VMEM((tok, 256), f32),
+            pltpu.VMEM((tok, 256), f32), pltpu.VMEM((tok, 128), f32),
+            pltpu.VMEM((blocks, 128, Q), bf16), pltpu.VMEM((blocks, 128, Q), bf16),
         ],
         compiler_params=arbitrary,
         cost_estimate=cost(2 * 10**10, 10**7),
         name="pairs",
-    )(inputs, out_grad, b_proj, c_proj, bt, ct, cols, scales, info)
+    )(inputs, out_grad, b_proj, c_proj, scales, info)
     sums, gb = lax.optimization_barrier((sums, gb))
     carried, *starts = pl.pallas_call(
         carry_kernel,
@@ -492,29 +501,42 @@
     gc = lax.all_to_all(
         gc.reshape(4, tok // 4, 128), "head", split_axis=0, concat_axis=0, tiled=True
     ).sum(axis=0)
-    grad_inputs, grad_step_raw, *gbs = pl.pallas_call(
+    through, *gbs = pl.pallas_call(
         backward_kernel,
         grid=(4,),
         in_specs=[
-            quarter, narrow, narrow, whole((4, 16, tok)), states,
-            block, narrow, rows8,
-            rows8, state,
+            quarter, narrow, states, narrow, state,
             pl.BlockSpec((16, 1, 16, 128), lambda g: (0, g // 2, g % 2, 0)),
         ],
-        out_specs=[quarter, whole((16, tok))] + [whole((tok // 4, 128))] * 4,
-        out_shape=[shape(tok, 1024, dtype=bf16), shape(16, tok)] + [shape(tok // 4, 128)] * 4,
-        scratch_shapes=[
-            pltpu.VMEM((tok, 128), f32), pltpu.VMEM((4, 8, tok), f32), pltpu.VMEM((4, 4, Q), f32), pltpu.VMEM((tok, 256), f32)
-        ],
+        out_specs=[pl.BlockSpec((1, 8, 128), lambda g: (g, 0, 0))] + [whole((tok // 4, 128))] * 4,
+        out_shape=[shape(4, 8, 128)] + [shape(tok // 4, 128)] * 4,
+        scratch_shapes=[pltpu.VMEM((tok, 128), f32), pltpu.VMEM((tok, 256), f32)],
         compiler_params=arbitrary,
         cost_estimate=cost(3 * 10**9, 10**7),
         name="backward",
+    )(inputs, scales, back, gb, end, incoming.reshape(16, 2, 32, 128))
+    moved = []
+    for d, part in enumerate(gbs):
+        moved.append(around(part, d))
+    grad_inputs, grad_step_raw = pl.pallas_call(
+        last_kernel,
+        grid=(4,),
+        in_specs=[
+            quarter, narrow, narrow, whole((4, 24, tok)), block, rows8, rows8, states,
+            pl.BlockSpec((16, 1, 16, 128), lambda g: (0, g // 2, g % 2, 0)),
+            whole((4, 8, 128)),
+        ],
+        out_specs=[quarter, whole((16, tok))],
+        out_shape=[shape(tok, 1024, dtype=bf16), shape(16, tok)],
+        scratch_shapes=[pltpu.VMEM((4, 8, tok), f32), pltpu.VMEM((tok, 256), f32)],
+        compiler_params=arbitrary,
+        cost_estimate=cost(3 * 10**9, 10**7),
+        name="last",
     )(
-        inputs, b_proj, scales, info, back, adj, gb, pair_rows, rows,
-        end, incoming.reshape(16, 2, 32, 128),
+        inputs, b_proj, scales, info, adj, pair_rows, rows, back,
+        incoming.reshape(16, 2, 32, 128), through,
     )
-    far = around(gbs[2], 2)
-    gb = gbs[0] + around(gbs[1], 1) + around(gbs[3], 3) + far
+    gb = moved[0] + moved[1] + moved[3] + moved[2]
     return grad_inputs, grad_step_raw.T, gb, gc
 
 

time: 85.1 us -> 85.5 us (level)
  the two profiles are of different devices: /device:TPU:1 before, /device:TPU:2 now
where the time goes in v1:
time: 85.5 us; the launch traced here: 84.8 us
  Pallas kernels  44.2 us (52%)
  starting transfers between devices  30.2 us (35%)
  waiting for transfers between devices  7 us (8%)
  other arithmetic  1.37 us (2%)
  local copies, waits for them, and re-layouts  1.36 us (2%)
    pallas_call x1, Pallas kernels, on_device(): pl.pallas_call(pair_kernel, grid=(4,), in_specs=[quarter, quarter, narrow...  13.8 us
    ppermute x6, starting transfers between devices, around(): lax.ppermute(array, 'head', [(i, (i + distance) % heads) for i in range(h...  11.5 us
    all_to_all x1, starting transfers between devices, on_device(): sums = lax.all_to_all(sums, 'seq', split_axis=0, concat_axis=0, tiled=True)  8.46 us
    pallas_call x1, Pallas kernels, on_device(): pl.pallas_call(last_kernel, grid=(4,), in_specs=[quarter, narrow, narrow,...  7.97 us
    pallas_call x1, Pallas kernels, on_device(): pl.pallas_call(forward_kernel, grid=(4,), in_specs=[quarter, narrow, stat...  7.67 us
    pallas_call x1, Pallas kernels, on_device(): pl.pallas_call(backward_kernel, grid=(4,), in_specs=[quarter, narrow, sta...  7.27 us
    pallas_call x1, Pallas kernels, on_device(): pl.pallas_call(first_kernel, grid=(4,), in_specs=[pl.BlockSpec(memory_spa...  6.66 us
    all_to_all x1, starting transfers between devices, on_device(): lax.all_to_all(carried, 'seq', split_axis=0, concat_axis=0, tiled=True)  6.42 us
  transfers between devices with their start and end apart: 9, of which 3 were waited for; matrix products, arithmetic and copies ran while one was open for 1% of the time, Pallas kernels for 43%

profile of v1, /device:TPU:2, one launch (start us, length us, event | category | flops | bytes accessed | tf_op | source)
XLA Modules:
  0.0 84.8 jit_solution(2227360845737467369)
XLA Ops:
  0.6 6.7 %first.1 = (f32[32,72,128]{2,1,0:T(8,128)}, bf16[1024,128]{1,0:T(8,128)(2,1)}, f32[4,24,1024]{2,1,0:T(8,128)}) custom-call(s32[32]{0:T(128)} %slot_ref.1, f32[16,1024]{1,0:T(8,128)} %bitcast.12, f32[1,16]{1,0:T(1,128)} %bitcast.14, f32[1,16]{1,0:T(1,128)} %bitcast.15, f32[1,16]{1,0:T(1,128)} %bitcast.16, bf16[1024,1024]{1,0:T(8,128)(2,1)} %dy_ref.5, ...), custom_call_target="tpu_custom_call" | custom-call | flops 1000000000 | bytes 10000000 | tf_op jit(solution)/shard_map/first/pallas_call | solution.py:427
  7.3 8.5 %all-to-all-start = ((f32[32,72,128]{2,1,0:T(8,128)}), f32[32,72,128]{2,1,0:T(8,128)S(1)}, u32[]{:S(2)}, u32[]{:S(2)}) async-start(f32[32,72,128]{2,1,0:T(8,128)} %get-tuple-element.35), calls=%async_computation | async-start | bytes 2359296 | tf_op jit(solution)/shard_map/all_to_all | solution.py:446
  15.8 13.8 %pairs.1 = (f32[4,1024,256]{2,1,0:T(8,128)}, f32[4,8,1024]{2,1,0:T(8,128)}, f32[4,8,128,256]{3,2,1,0:T(8,128)}, f32[4,8,128,256]{3,2,1,0:T(8,128)}, f32[1024,128]{1,0:T(8,128)}, /*index=5*/f32[1024,128]{1,0:T(8,128)}) custom-call(bf16[1024,1024]{1,0:T(8,128)(2,1)} %x_ref.5, bf16[1024,1024]{1,0:T(8,128)(2,1)} %dy_ref.5, bf16[1024,128]{1,0:T(8,128)(2,1)} %b_ref.3, ...), custom_call_target="tpu_custom_call" | custom-call | flops 20000000000 | bytes 10000000 | tf_op jit(solution)/shard_map/pairs/pallas_call | solution.py:448
  29.5 2.0 %all-to-all-done.sums_ref = f32[32,72,128]{2,1,0:T(8,128)S(1)} async-done(((f32[32,72,128]{2,1,0:T(8,128)}), f32[32,72,128]{2,1,0:T(8,128)S(1)}, u32[]{:S(2)}, u32[]{:S(2)}) %all-to-all-start) | async-done | bytes 1179680 | tf_op jit(solution)/shard_map/all_to_all | solution.py:446
  31.6 0.9 %carry.1 = (f32[32,32,128]{2,1,0:T(8,128)}, f32[8,32,128]{2,1,0:T(8,128)S(1)}, f32[8,32,128]{2,1,0:T(8,128)S(1)}, f32[8,32,128]{2,1,0:T(8,128)S(1)}, f32[8,32,128]{2,1,0:T(8,128)S(1)}) custom-call(f32[32,72,128]{2,1,0:T(8,128)S(1)} %all-to-all-done.sums_ref), custom_call_target="tpu_custom_call" | custom-call | flops 1000000 | bytes 1000000 | tf_op jit(solution)/shard_map/carry/pallas_call | solution.py:469
  32.4 0.7 copy-done
  33.1 6.4 %all-to-all-start.1 = ((f32[32,32,128]{2,1,0:T(8,128)}), f32[32,32,128]{2,1,0:T(8,128)S(1)}, u32[]{:S(2)}, u32[]{:S(2)}) async-start(f32[32,32,128]{2,1,0:T(8,128)} %get-tuple-element.45), calls=%async_computation.1 | async-start | bytes 1048576 | tf_op jit(solution)/shard_map/all_to_all | solution.py:482
  39.5 1.6 %collective-permute-start = (f32[8,32,128]{2,1,0:T(8,128)S(1)}, f32[8,32,128]{2,1,0:T(8,128)S(1)}, u32[]{:S(2)}, u32[]{:S(2)}) collective-permute-start(f32[8,32,128]{2,1,0:T(8,128)S(1)} %get-tuple-element.39), channel_id=1, source_target_pairs={{0,1},{1,2},{2,3},{3,0},{4,5},{5,6},{6,7},{7,4},{8,9},{9,10},{10,1... | collective-permute-start | bytes 393224 | tf_op jit(solution)/shard_map/ppermute | solution.py:401
  41.2 2.9 %collective-permute-start.1 = (f32[8,32,128]{2,1,0:T(8,128)S(1)}, f32[8,32,128]{2,1,0:T(8,128)S(1)}, u32[]{:S(2)}, u32[]{:S(2)}) collective-permute-start(f32[8,32,128]{2,1,0:T(8,128)S(1)} %get-tuple-element.40), channel_id=1, source_target_pairs={{0,2},{1,3},{2,0},{3,1},{4,6},{5,7},{6,4},{7,5},{8,10},{9,11},{10,... | collective-permute-start | bytes 393224 | tf_op jit(solution)/shard_map/ppermute | solution.py:401
  44.1 1.3 %collective-permute-start.2 = (f32[8,32,128]{2,1,0:T(8,128)S(1)}, f32[8,32,128]{2,1,0:T(8,128)S(1)}, u32[]{:S(2)}, u32[]{:S(2)}) collective-permute-start(f32[8,32,128]{2,1,0:T(8,128)S(1)} %get-tuple-element.41), channel_id=1, source_target_pairs={{0,3},{1,0},{2,1},{3,2},{4,7},{5,4},{6,5},{7,6},{8,11},{9,8},{10,9... | collective-permute-start | bytes 393224 | tf_op jit(solution)/shard_map/ppermute | solution.py:401
  45.4 1.0 %collective-permute-done.start1_ref = f32[8,32,128]{2,1,0:T(8,128)S(1)} collective-permute-done((f32[8,32,128]{2,1,0:T(8,128)S(1)}, f32[8,32,128]{2,1,0:T(8,128)S(1)}, u32[]{:S(2)}, u32[]{:S(2)}) %collective-permute-start) | collective-permute-done | bytes 131104 | tf_op jit(solution)/shard_map/ppermute | solution.py:401
  46.4 4.0 %collective-permute-done.1.start2_ref = f32[8,32,128]{2,1,0:T(8,128)S(1)} collective-permute-done((f32[8,32,128]{2,1,0:T(8,128)S(1)}, f32[8,32,128]{2,1,0:T(8,128)S(1)}, u32[]{:S(2)}, u32[]{:S(2)}) %collective-permute-start.1) | collective-permute-done | bytes 131104 | tf_op jit(solution)/shard_map/ppermute | solution.py:401
  50.4 0.0 collective-permute-done.2.start3_ref
  50.4 0.6 copy-done.4
  51.0 0.1 copy-done.5
  51.1 7.7 %forward.1 = (f32[1024,128]{1,0:T(8,128)}, f32[4,8,1024]{2,1,0:T(8,128)}, f32[4,128,256]{2,1,0:T(8,128)}) custom-call(bf16[1024,1024]{1,0:T(8,128)(2,1)} %dy_ref.5, bf16[1024,128]{1,0:T(8,128)(2,1)} %c_ref.5, f32[4,8,128,256]{3,2,1,0:T(8,128)} %get-tuple-element.34.into_ref, bf16[1024,128]{1,0:T(8,128)(2,1)} %get-tuple-element.30.scales_ref, ...), custom_call_target="tpu_custom_call" | custom-call | flops 3000000000 | bytes 10000000 | tf_op jit(solution)/shard_map/forward/pallas_call | solution.py:483
  58.8 3.8 %all-to-all-start.2 = ((f32[4,256,128]{2,1,0:T(8,128)}), f32[4,256,128]{2,1,0:T(8,128)S(1)}, u32[]{:S(2)}, u32[]{:S(2)}) async-start(f32[4,256,128]{2,1,0:T(8,128)} %bitcast.10), calls=%async_computation.2 | async-start | bytes 1048576 | tf_op jit(solution)/shard_map/all_to_all | solution.py:501
  62.6 7.3 %backward.1 = (f32[4,8,128]{2,1,0:T(8,128)}, f32[256,128]{1,0:T(8,128)}, f32[256,128]{1,0:T(8,128)}, f32[256,128]{1,0:T(8,128)}, f32[256,128]{1,0:T(8,128)}) custom-call(bf16[1024,1024]{1,0:T(8,128)(2,1)} %x_ref.5, bf16[1024,128]{1,0:T(8,128)(2,1)} %get-tuple-element.30.scales_ref, f32[4,8,128,256]{3,2,1,0:T(8,128)} %get-tuple-element.44.back_ref, ...), custom_call_target="tpu_custom_call" | custom-call | flops 3000000000 | bytes 10000000 | tf_op jit(solution)/shard_map/backward/pallas_call | solution.py:504
  69.8 2.1 %collective-permute-start.3 = (f32[256,128]{1,0:T(8,128)}, f32[256,128]{1,0:T(8,128)S(1)}, u32[]{:S(2)}, u32[]{:S(2)}) collective-permute-start(f32[256,128]{1,0:T(8,128)} %get-tuple-element.52), channel_id=1, source_target_pairs={{0,1},{1,2},{2,3},{3,0},{4,5},{5,6},{6,7},{7,4},{8,9},{9,10},{10,1... | collective-permute-start | bytes 393224 | tf_op jit(solution)/shard_map/ppermute | solution.py:401
  71.9 1.3 %collective-permute-start.4 = (f32[256,128]{1,0:T(8,128)}, f32[256,128]{1,0:T(8,128)S(1)}, u32[]{:S(2)}, u32[]{:S(2)}) collective-permute-start(f32[256,128]{1,0:T(8,128)} %get-tuple-element.53), channel_id=1, source_target_pairs={{0,3},{1,0},{2,1},{3,2},{4,7},{5,4},{6,5},{7,6},{8,11},{9,8},{10,9... | collective-permute-start | bytes 393224 | tf_op jit(solution)/shard_map/ppermute | solution.py:401
  73.2 2.2 %collective-permute-start.5 = (f32[256,128]{1,0:T(8,128)}, f32[256,128]{1,0:T(8,128)S(1)}, u32[]{:S(2)}, u32[]{:S(2)}) collective-permute-start(f32[256,128]{1,0:T(8,128)} %get-tuple-element.54), channel_id=1, source_target_pairs={{0,2},{1,3},{2,0},{3,1},{4,6},{5,7},{6,4},{7,5},{8,10},{9,11},{10,... | collective-permute-start | bytes 393224 | tf_op jit(solution)/shard_map/ppermute | solution.py:401
  75.5 8.0 %last.1 = (bf16[1024,1024]{1,0:T(8,128)(2,1)}, f32[16,1024]{1,0:T(8,128)}) custom-call(bf16[1024,1024]{1,0:T(8,128)(2,1)} %x_ref.5, bf16[1024,128]{1,0:T(8,128)(2,1)} %b_ref.3, bf16[1024,128]{1,0:T(8,128)(2,1)} %get-tuple-element.30.scales_ref, f32[4,24,1024]{2,1,0:T(8,128)} %get-tuple-element.31.info_ref, f32[4,1024,256]{2,1,0:T(8,128)} %get-tuple-element.32.adj_ref, ...), custom_call_target="tpu_custom_call" | custom-call | flops 3000000000 | bytes 10000000 | tf_op jit(solution)/shard_map/last/pallas_call | solution.py:521
  83.5 0.7 reduce_sum.9
  84.2 0.7 add_add_fusion
  (14 shorter events, 0.0 us)
Async XLA Ops:
  7.3 24.3 %all-to-all-start = ((f32[32,72,128]{2,1,0:T(8,128)}), f32[32,72,128]{2,1,0:T(8,128)S(1)}, u32[]{:S(2)}, u32[]{:S(2)}) async-start(f32[32,72,128]{2,1,0:T(8,128)} %get-tuple-element.35), calls=%async_computation | async-start | bytes 2359296 | tf_op jit(solution)/shard_map/all_to_all | solution.py:446
  32.4 0.7 copy-start
  33.1 25.7 %all-to-all-start.1 = ((f32[32,32,128]{2,1,0:T(8,128)}), f32[32,32,128]{2,1,0:T(8,128)S(1)}, u32[]{:S(2)}, u32[]{:S(2)}) async-start(f32[32,32,128]{2,1,0:T(8,128)} %get-tuple-element.45), calls=%async_computation.1 | async-start | bytes 1048576 | tf_op jit(solution)/shard_map/all_to_all | solution.py:482
  39.5 6.9 %collective-permute-start = (f32[8,32,128]{2,1,0:T(8,128)S(1)}, f32[8,32,128]{2,1,0:T(8,128)S(1)}, u32[]{:S(2)}, u32[]{:S(2)}) collective-permute-start(f32[8,32,128]{2,1,0:T(8,128)S(1)} %get-tuple-element.39), channel_id=1, source_target_pairs={{0,1},{1,2},{2,3},{3,0},{4,5},{5,6},{6,7},{7,4},{8,9},{9,10},{10,1... | collective-permute-start | bytes 393224 | tf_op jit(solution)/shard_map/ppermute | solution.py:401
  41.2 9.2 %collective-permute-start.1 = (f32[8,32,128]{2,1,0:T(8,128)S(1)}, f32[8,32,128]{2,1,0:T(8,128)S(1)}, u32[]{:S(2)}, u32[]{:S(2)}) collective-permute-start(f32[8,32,128]{2,1,0:T(8,128)S(1)} %get-tuple-element.40), channel_id=1, source_target_pairs={{0,2},{1,3},{2,0},{3,1},{4,6},{5,7},{6,4},{7,5},{8,10},{9,11},{10,... | collective-permute-start | bytes 393224 | tf_op jit(solution)/shard_map/ppermute | solution.py:401
  44.1 6.3 %collective-permute-start.2 = (f32[8,32,128]{2,1,0:T(8,128)S(1)}, f32[8,32,128]{2,1,0:T(8,128)S(1)}, u32[]{:S(2)}, u32[]{:S(2)}) collective-permute-start(f32[8,32,128]{2,1,0:T(8,128)S(1)} %get-tuple-element.41), channel_id=1, source_target_pairs={{0,3},{1,0},{2,1},{3,2},{4,7},{5,4},{6,5},{7,6},{8,11},{9,8},{10,9... | collective-permute-start | bytes 393224 | tf_op jit(solution)/shard_map/ppermute | solution.py:401
  46.4 4.0 %copy-start.3 = (f32[8,32,128]{2,1,0:T(8,128)}, f32[8,32,128]{2,1,0:T(8,128)S(1)}, u32[]{:S(2)}) copy-start(f32[8,32,128]{2,1,0:T(8,128)S(1)} %collective-permute-done.start1_ref) | copy-start | bytes 393220
  50.4 0.6 copy-start.4
  50.4 0.7 copy-start.5
  58.8 3.8 %copy-start.1 = (f32[32,32,128]{2,1,0:T(8,128)}, f32[32,32,128]{2,1,0:T(8,128)S(1)}, u32[]{:S(2)}) copy-start(f32[32,32,128]{2,1,0:T(8,128)S(1)} %all-to-all-done.1) | copy-start | bytes 1572868
  58.8 24.7 %all-to-all-start.2 = ((f32[4,256,128]{2,1,0:T(8,128)}), f32[4,256,128]{2,1,0:T(8,128)S(1)}, u32[]{:S(2)}, u32[]{:S(2)}) async-start(f32[4,256,128]{2,1,0:T(8,128)} %bitcast.10), calls=%async_computation.2 | async-start | bytes 1048576 | tf_op jit(solution)/shard_map/all_to_all | solution.py:501
  69.8 14.3 %collective-permute-start.3 = (f32[256,128]{1,0:T(8,128)}, f32[256,128]{1,0:T(8,128)S(1)}, u32[]{:S(2)}, u32[]{:S(2)}) collective-permute-start(f32[256,128]{1,0:T(8,128)} %get-tuple-element.52), channel_id=1, source_target_pairs={{0,1},{1,2},{2,3},{3,0},{4,5},{5,6},{6,7},{7,4},{8,9},{9,10},{10,1... | collective-permute-start | bytes 393224 | tf_op jit(solution)/shard_map/ppermute | solution.py:401
  71.9 12.2 %collective-permute-start.4 = (f32[256,128]{1,0:T(8,128)}, f32[256,128]{1,0:T(8,128)S(1)}, u32[]{:S(2)}, u32[]{:S(2)}) collective-permute-start(f32[256,128]{1,0:T(8,128)} %get-tuple-element.53), channel_id=1, source_target_pairs={{0,3},{1,0},{2,1},{3,2},{4,7},{5,4},{6,5},{7,6},{8,11},{9,8},{10,9... | collective-permute-start | bytes 393224 | tf_op jit(solution)/shard_map/ppermute | solution.py:401
  73.2 10.9 %collective-permute-start.5 = (f32[256,128]{1,0:T(8,128)}, f32[256,128]{1,0:T(8,128)S(1)}, u32[]{:S(2)}, u32[]{:S(2)}) collective-permute-start(f32[256,128]{1,0:T(8,128)} %get-tuple-element.54), channel_id=1, source_target_pairs={{0,2},{1,3},{2,0},{3,1},{4,6},{5,7},{6,4},{7,5},{8,10},{9,11},{10,... | collective-permute-start | bytes 393224 | tf_op jit(solution)/shard_map/ppermute | solution.py:401
  75.5 8.7 %copy-start.2 = (f32[256,128]{1,0:T(8,128)S(1)}, f32[256,128]{1,0:T(8,128)}, u32[]{:S(2)}) copy-start(f32[256,128]{1,0:T(8,128)} %get-tuple-element.51) | copy-start | bytes 393220

commit v2 on v1

--- a/solution.py
+++ b/solution.py
@@ -172,7 +172,8 @@
 
 def pair_kernel(
     x_ref, dy_ref, b_ref, c_ref, scales_ref, info_ref,
-    adj_ref, rows_ref, into_ref, back_ref, gb_ref, gc_ref,
+    adj_ref, rows_ref, into_ref, back_ref, xhigh_ref, xlow_ref, dyhigh_ref, dylow_ref, decay_ref,
+    gb_ref, gc_ref,
     tot_ref, meet_ref, scale_ref, cols_ref, bt_ref, ct_ref,
 ):
     g = pl.program_id(0)
@@ -193,16 +194,19 @@
         tot_ref[...] = jnp.zeros_like(tot_ref)
 
     skip = spread(group_cols(cols_ref[0:8, :], g), SKIP)[0:1, :]
-    for source_ref, base, turn_ref, out_ref in (
-        (x_ref, SHRINK, bt_ref, into_ref),
-        (dy_ref, GROW, ct_ref, back_ref),
+    for source_ref, base, turn_ref, out_ref, high_ref, low_ref in (
+        (x_ref, SHRINK, bt_ref, into_ref, xhigh_ref, xlow_ref),
+        (dy_ref, GROW, ct_ref, back_ref, dyhigh_ref, dylow_ref),
     ):
         scale_ref[...] = dn(scales_ref[...], repeater(base, g))
         for k in range(blocks):
             rows = slice(k * Q, (k + 1) * Q)
             high, low = split(source_ref[rows, :].astype(f32) * scale_ref[rows, :])
+            high_ref[0, rows, :] = high
+            low_ref[0, rows, :] = low
             turn = turn_ref[k]
             out_ref[0, k] = dn(side(turn, turn), stack(high, low))
+    decay_ref[0] = stack(*[scale_ref[k * Q + Q - 1 : k * Q + Q, :] for k in range(blocks)])
 
     upper = lax.broadcasted_iota(jnp.int32, (Q, Q), 0) <= lax.broadcasted_iota(
         jnp.int32, (Q, Q), 1
@@ -271,12 +275,12 @@
 
 
 def forward_kernel(
-    dy_ref, c_ref, into_ref, scales_ref, start0_ref, start1_ref, start2_ref, start3_ref, gc_in_ref,
+    dyhigh_ref, dylow_ref, c_ref, into_ref, decay_ref, start0_ref, start1_ref, start2_ref, start3_ref, gc_in_ref,
     gc_ref, rows_ref, end_ref,
-    hold_ref, grow_ref,
+    hold_ref,
 ):
     g = pl.program_id(0)
-    blocks = dy_ref.shape[0] // Q
+    blocks = c_ref.shape[0] // Q
 
     @pl.when(g == 0)
     def copy():
@@ -290,28 +294,26 @@
             to = pl.ds(pl.multiple_of(64 * h + 16 * part, 16), 16)
             hold_ref[to, :] = start_ref[h // 2, at : at + 16, :]
     state = hold_ref[...].T
-    grow_ref[...] = dn(scales_ref[...], repeater(GROW, g))
     for k in range(blocks):
         rows = slice(k * Q, (k + 1) * Q)
-        grow = grow_ref[rows, :]
         s_high, s_low = split(state)
         c = c_ref[rows, :]
         from_state = dn(side(c, c), stack(s_high, s_low))
-        dy_grown = dy_ref[rows, :].astype(f32) * grow
-        dy_high, dy_low = split(dy_grown)
+        dy_high, dy_low = dyhigh_ref[0, rows, :], dylow_ref[0, rows, :]
+        dy_grown = dy_high.astype(f32) + dy_low.astype(f32)
         rows_ref[0, 0:4, rows] = head_sums(dy_grown * from_state)
         gc_ref[rows, :] += three(dy_high, dy_low, s_high, s_low)
-        state = grow[Q - 1 : Q, :] * state + into_ref[0, k]
+        state = decay_ref[0, k : k + 1, :] * state + into_ref[0, k]
     end_ref[0] = state
 
 
 def backward_kernel(
-    x_ref, scales_ref, back_ref, gb_in_ref, end_ref, in_ref,
+    xhigh_ref, xlow_ref, decay_ref, back_ref, gb_in_ref, end_ref, in_ref,
     through_ref, gb0_ref, gb1_ref, gb2_ref, gb3_ref,
-    gb_ref, shrink_ref,
+    gb_ref,
 ):
     g = pl.program_id(0)
-    blocks = x_ref.shape[0] // Q
+    blocks = gb_ref.shape[0] // Q
 
     @pl.when(g == 0)
     def copy():
@@ -323,15 +325,12 @@
     lane = lax.broadcasted_iota(jnp.int32, (8, 256), 1)
     through = jnp.sum(jnp.where(row == lane // 64, meeting, 0.0), axis=1, keepdims=True)
     through_ref[0] = jnp.broadcast_to(through, (8, 128))
-    shrink_ref[...] = dn(scales_ref[...], repeater(SHRINK, g))
-    ends = stack(*[scales_ref[k * Q + Q - 16 : k * Q + Q, :] for k in range(blocks)])
-    decays = dn(ends, repeater(GROW, g))
     for k in reversed(range(blocks)):
         rows = slice(k * Q, (k + 1) * Q)
-        x_high, x_low = split(x_ref[rows, :].astype(f32) * shrink_ref[rows, :])
+        x_high, x_low = xhigh_ref[0, rows, :], xlow_ref[0, rows, :]
         g_high, g_low = split(adjoint)
         gb_ref[rows, :] += three(x_high, x_low, g_high, g_low)
-        adjoint = decays[16 * k + 15 : 16 * k + 16, :] * adjoint + back_ref[0, k]
+        adjoint = decay_ref[0, k : k + 1, :] * adjoint + back_ref[0, k]
 
     @pl.when(g == pl.num_programs(0) - 1)
     def finish():
@@ -344,7 +343,7 @@
 
 def last_kernel(
     x_ref, b_ref, scales_ref, info_ref, adj_ref, pair_rows_ref, rows_ref,
-    back_ref, in_ref, through_ref,
+    back_ref, decay_ref, in_ref, through_ref,
     gx_ref, raw_ref,
     keep_ref, shrink_ref,
 ):
@@ -352,13 +351,11 @@
     blocks = x_ref.shape[0] // Q
     adjoint = side(*[in_ref[:, 0, 8 * r : 8 * r + 8, :].reshape(128, 128) for r in range(2)])
     shrink_ref[...] = dn(scales_ref[...], repeater(SHRINK, g))
-    ends = stack(*[scales_ref[k * Q + Q - 16 : k * Q + Q, :] for k in range(blocks)])
-    decays = dn(ends, repeater(GROW, g))
     for k in reversed(range(blocks)):
         rows = slice(k * Q, (k + 1) * Q)
         b = b_ref[rows, :]
         adj = shrink_ref[rows, :] * dn(side(b, b), stack(*split(adjoint)))
-        adjoint = decays[16 * k + 15 : 16 * k + 16, :] * adjoint + back_ref[0, k]
+        adjoint = decay_ref[0, k : k + 1, :] * adjoint + back_ref[0, k]
         gx_ref[rows, :] = (adj_ref[0, rows, :] + adj).astype(bf16)
         out_rows = pair_rows_ref[0, 4:8, rows] + head_sums(x_ref[rows, :].astype(f32) * adj)
         keep_ref[g, 0:4, rows] = (
@@ -423,6 +420,7 @@
     rows8 = pl.BlockSpec((1, 8, tok), lambda g: (g, 0, 0))
     states = pl.BlockSpec((1, blocks, 128, 256), lambda g: (g, 0, 0, 0))
     block = pl.BlockSpec((1, tok, 256), lambda g: (g, 0, 0))
+    ends = pl.BlockSpec((1, blocks, 256), lambda g: (g, 0, 0))
     state = pl.BlockSpec((1, 128, 256), lambda g: (g, 0, 0))
     sums, scales, info = pl.pallas_call(
         first_kernel,
@@ -445,16 +443,17 @@
     )
     sums = lax.all_to_all(sums, "seq", split_axis=0, concat_axis=0, tiled=True)
 
-    adj, pair_rows, into, back, gb, gc = pl.pallas_call(
+    adj, pair_rows, into, back, x_high, x_low, dy_high, dy_low, decays, gb, gc = pl.pallas_call(
         pair_kernel,
         grid=(4,),
         in_specs=[
             quarter, quarter, narrow, narrow, narrow, whole((4, 24, tok))
         ],
-        out_specs=[block, rows8, states, states, narrow, narrow],
+        out_specs=[block, rows8, states, states] + [block] * 4 + [ends, narrow, narrow],
         out_shape=[
             shape(4, tok, 256), shape(4, 8, tok), shape(4, blocks, 128, 256),
-            shape(4, blocks, 128, 256), shape(tok, 128), shape(tok, 128),
+            shape(4, blocks, 128, 256), *[shape(4, tok, 256, dtype=bf16)] * 4,
+            shape(4, blocks, 256), shape(tok, 128), shape(tok, 128),
         ],
         scratch_shapes=[
             pltpu.VMEM((blocks, Q, Q), f32), pltpu.VMEM((blocks, Q, Q), f32),
@@ -471,7 +470,7 @@
         grid=(1,),
         in_specs=[whole((segs, 72, 128))],
         out_specs=[whole((segs, 32, 128))] + [whole((8, 32, 128))] * 4,
-        out_shape=[shape(segs, 32, 128)] + [shape(8, 32, 128)] * 4,
+        out_shape=[pltpu.HBM((segs, 32, 128), f32)] + [pltpu.HBM((8, 32, 128), f32)] * 4,
         compiler_params=pltpu.CompilerParams(vmem_limit_bytes=8 * 2**20),
         cost_estimate=cost(10**6, 10**6),
         name="carry",
@@ -484,7 +483,7 @@
         forward_kernel,
         grid=(4,),
         in_specs=[
-            quarter, narrow, states, narrow,
+            block, block, narrow, states, ends,
             *[pl.BlockSpec((2, 32, 128), lambda g: (g, 0, 0))] * 4, narrow,
         ],
         out_specs=[narrow, rows8, state],
@@ -492,12 +491,12 @@
             shape(tok, 128), shape(4, 8, tok), shape(4, 128, 256),
         ),
         scratch_shapes=[
-            pltpu.VMEM((256, 128), f32), pltpu.VMEM((tok, 256), f32)
+            pltpu.VMEM((256, 128), f32),
         ],
         compiler_params=arbitrary,
         cost_estimate=cost(3 * 10**9, 10**7),
         name="forward",
-    )(out_grad, c_proj, into, scales, *shifted, gc)
+    )(dy_high, dy_low, c_proj, into, decays, *shifted, gc)
     gc = lax.all_to_all(
         gc.reshape(4, tok // 4, 128), "head", split_axis=0, concat_axis=0, tiled=True
     ).sum(axis=0)
@@ -505,16 +504,16 @@
         backward_kernel,
         grid=(4,),
         in_specs=[
-            quarter, narrow, states, narrow, state,
+            block, block, ends, states, narrow, state,
             pl.BlockSpec((16, 1, 16, 128), lambda g: (0, g // 2, g % 2, 0)),
         ],
         out_specs=[pl.BlockSpec((1, 8, 128), lambda g: (g, 0, 0))] + [whole((tok // 4, 128))] * 4,
         out_shape=[shape(4, 8, 128)] + [shape(tok // 4, 128)] * 4,
-        scratch_shapes=[pltpu.VMEM((tok, 128), f32), pltpu.VMEM((tok, 256), f32)],
+        scratch_shapes=[pltpu.VMEM((tok, 128), f32)],
         compiler_params=arbitrary,
         cost_estimate=cost(3 * 10**9, 10**7),
         name="backward",
-    )(inputs, scales, back, gb, end, incoming.reshape(16, 2, 32, 128))
+    )(x_high, x_low, decays, back, gb, end, incoming.reshape(16, 2, 32, 128))
     moved = []
     for d, part in enumerate(gbs):
         moved.append(around(part, d))
@@ -522,7 +521,7 @@
         last_kernel,
         grid=(4,),
         in_specs=[
-            quarter, narrow, narrow, whole((4, 24, tok)), block, rows8, rows8, states,
+            quarter, narrow, narrow, whole((4, 24, tok)), block, rows8, rows8, states, ends,
             pl.BlockSpec((16, 1, 16, 128), lambda g: (0, g // 2, g % 2, 0)),
             whole((4, 8, 128)),
         ],
@@ -533,7 +532,7 @@
         cost_estimate=cost(3 * 10**9, 10**7),
         name="last",
     )(
-        inputs, b_proj, scales, info, adj, pair_rows, rows, back,
+        inputs, b_proj, scales, info, adj, pair_rows, rows, back, decays,
         incoming.reshape(16, 2, 32, 128), through,
     )
     gb = moved[0] + moved[1] + moved[3] + moved[2]

time: 85.5 us -> 83.7 us (0.979)
    pallas_call x2, Pallas kernels: 14.9 us -> 13.7 us  [the longest x1 7.34 us: on_device(): pl.pallas_call(forward_kernel, grid=(4,), in_specs=[block, block, narrow,...]
where the time goes in v2:
time: 83.7 us; the launch traced here: 83.2 us
  Pallas kernels  43.6 us (52%)
  starting transfers between devices  30.2 us (36%)
  waiting for transfers between devices  6.52 us (8%)
  other arithmetic  1.37 us (2%)
    pallas_call x1, Pallas kernels, on_device(): pl.pallas_call(pair_kernel, grid=(4,), in_specs=[quarter, quarter, narrow...  14.5 us
    ppermute x6, starting transfers between devices, around(): lax.ppermute(array, 'head', [(i, (i + distance) % heads) for i in range(h...  11.5 us
    all_to_all x1, starting transfers between devices, on_device(): sums = lax.all_to_all(sums, 'seq', split_axis=0, concat_axis=0, tiled=True)  8.46 us
    pallas_call x1, Pallas kernels, on_device(): pl.pallas_call(last_kernel, grid=(4,), in_specs=[quarter, narrow, narrow,...  7.72 us
    pallas_call x1, Pallas kernels, on_device(): pl.pallas_call(forward_kernel, grid=(4,), in_specs=[block, block, narrow,...  7.34 us
    pallas_call x1, Pallas kernels, on_device(): pl.pallas_call(first_kernel, grid=(4,), in_specs=[pl.BlockSpec(memory_spa...  6.67 us
    all_to_all x1, starting transfers between devices, on_device(): lax.all_to_all(carried, 'seq', split_axis=0, concat_axis=0, tiled=True)  6.42 us
    pallas_call x1, Pallas kernels, on_device(): pl.pallas_call(backward_kernel, grid=(4,), in_specs=[block, block, ends,...  6.36 us
  transfers between devices with their start and end apart: 9, of which 3 were waited for; matrix products, arithmetic and copies ran while one was open for 1% of the time, Pallas kernels for 43%

profile of v2, /device:TPU:2, one launch (start us, length us, event | category | flops | bytes accessed | tf_op | source)
XLA Modules:
  0.0 83.2 jit_solution(18035654749786520913)
XLA Ops:
  0.6 6.7 %first.1 = (f32[32,72,128]{2,1,0:T(8,128)}, bf16[1024,128]{1,0:T(8,128)(2,1)}, f32[4,24,1024]{2,1,0:T(8,128)}) custom-call(s32[32]{0:T(128)} %slot_ref.1, f32[16,1024]{1,0:T(8,128)} %bitcast.12, f32[1,16]{1,0:T(1,128)} %bitcast.14, f32[1,16]{1,0:T(1,128)} %bitcast.15, f32[1,16]{1,0:T(1,128)} %bitcast.16, bf16[1024,1024]{1,0:T(8,128)(2,1)} %dy_ref.3, ...), custom_call_target="tpu_custom_call" | custom-call | flops 1000000000 | bytes 10000000 | tf_op jit(solution)/shard_map/first/pallas_call | solution.py:425
  7.3 8.5 %all-to-all-start = ((f32[32,72,128]{2,1,0:T(8,128)}), f32[32,72,128]{2,1,0:T(8,128)S(1)}, u32[]{:S(2)}, u32[]{:S(2)}) async-start(f32[32,72,128]{2,1,0:T(8,128)} %get-tuple-element.43), calls=%async_computation | async-start | bytes 2359296 | tf_op jit(solution)/shard_map/all_to_all | solution.py:444
  15.8 14.5 %pairs.1 = (f32[4,1024,256]{2,1,0:T(8,128)}, f32[4,8,1024]{2,1,0:T(8,128)}, f32[4,8,128,256]{3,2,1,0:T(8,128)}, f32[4,8,128,256]{3,2,1,0:T(8,128)}, bf16[4,1024,...) custom-call(bf16[1024,1024]{1,0:T(8,128)(2,1)} %x_ref.3, ...), custom_call_target="tpu_custom_call" | custom-call | flops 20000000000 | bytes 10000000 | tf_op jit(solution)/shard_map/pairs/pallas_call | solution.py:446
  30.2 1.3 %all-to-all-done.sums_ref = f32[32,72,128]{2,1,0:T(8,128)S(1)} async-done(((f32[32,72,128]{2,1,0:T(8,128)}), f32[32,72,128]{2,1,0:T(8,128)S(1)}, u32[]{:S(2)}, u32[]{:S(2)}) %all-to-all-start) | async-done | bytes 1179680 | tf_op jit(solution)/shard_map/all_to_all | solution.py:444
  31.6 1.1 %carry.1 = (f32[32,32,128]{2,1,0:T(8,128)}, f32[8,32,128]{2,1,0:T(8,128)}, f32[8,32,128]{2,1,0:T(8,128)}, f32[8,32,128]{2,1,0:T(8,128)}, f32[8,32,128]{2,1,0:T(8,128)}) custom-call(f32[32,72,128]{2,1,0:T(8,128)S(1)} %all-to-all-done.sums_ref), custom_call_target="tpu_custom_call" | custom-call | flops 1000000 | bytes 1000000 | tf_op jit(solution)/shard_map/carry/pallas_call | solution.py:468
  32.7 6.4 %all-to-all-start.1 = ((f32[32,32,128]{2,1,0:T(8,128)}), f32[32,32,128]{2,1,0:T(8,128)S(1)}, u32[]{:S(2)}, u32[]{:S(2)}) async-start(f32[32,32,128]{2,1,0:T(8,128)} %get-tuple-element.53), calls=%async_computation.1 | async-start | bytes 1048576 | tf_op jit(solution)/shard_map/all_to_all | solution.py:481
  39.1 1.6 %collective-permute-start = (f32[8,32,128]{2,1,0:T(8,128)}, f32[8,32,128]{2,1,0:T(8,128)S(1)}, u32[]{:S(2)}, u32[]{:S(2)}) collective-permute-start(f32[8,32,128]{2,1,0:T(8,128)} %get-tuple-element.47), channel_id=1, source_target_pairs={{0,1},{1,2},{2,3},{3,0},{4,5},{5,6},{6,7},{7,4},{8,9},{9,10},{10,1... | collective-permute-start | bytes 393224 | tf_op jit(solution)/shard_map/ppermute | solution.py:398
  40.8 2.9 %collective-permute-start.1 = (f32[8,32,128]{2,1,0:T(8,128)}, f32[8,32,128]{2,1,0:T(8,128)S(1)}, u32[]{:S(2)}, u32[]{:S(2)}) collective-permute-start(f32[8,32,128]{2,1,0:T(8,128)} %get-tuple-element.48), channel_id=1, source_target_pairs={{0,2},{1,3},{2,0},{3,1},{4,6},{5,7},{6,4},{7,5},{8,10},{9,11},{10,... | collective-permute-start | bytes 393224 | tf_op jit(solution)/shard_map/ppermute | solution.py:398
  43.7 1.3 %collective-permute-start.2 = (f32[8,32,128]{2,1,0:T(8,128)}, f32[8,32,128]{2,1,0:T(8,128)S(1)}, u32[]{:S(2)}, u32[]{:S(2)}) collective-permute-start(f32[8,32,128]{2,1,0:T(8,128)} %get-tuple-element.49), channel_id=1, source_target_pairs={{0,3},{1,0},{2,1},{3,2},{4,7},{5,4},{6,5},{7,6},{8,11},{9,8},{10,9... | collective-permute-start | bytes 393224 | tf_op jit(solution)/shard_map/ppermute | solution.py:398
  45.0 1.2 %collective-permute-done.start1_ref = f32[8,32,128]{2,1,0:T(8,128)S(1)} collective-permute-done((f32[8,32,128]{2,1,0:T(8,128)}, f32[8,32,128]{2,1,0:T(8,128)S(1)}, u32[]{:S(2)}, u32[]{:S(2)}) %collective-permute-start) | collective-permute-done | bytes 131104 | tf_op jit(solution)/shard_map/ppermute | solution.py:398
  46.2 4.0 %collective-permute-done.1.start2_ref = f32[8,32,128]{2,1,0:T(8,128)S(1)} collective-permute-done((f32[8,32,128]{2,1,0:T(8,128)}, f32[8,32,128]{2,1,0:T(8,128)S(1)}, u32[]{:S(2)}, u32[]{:S(2)}) %collective-permute-start.1) | collective-permute-done | bytes 131104 | tf_op jit(solution)/shard_map/ppermute | solution.py:398
  50.2 0.0 collective-permute-done.2.start3_ref
  50.2 0.6 copy-done.3
  50.8 0.1 copy-done.4
  50.9 7.3 %forward.1 = (f32[1024,128]{1,0:T(8,128)}, f32[4,8,1024]{2,1,0:T(8,128)}, f32[4,128,256]{2,1,0:T(8,128)}) custom-call(bf16[4,1024,256]{2,1,0:T(8,128)(2,1)} %get-tuple-element.39.dyhigh_ref, bf16[4,1024,256]{2,1,0:T(8,128)(2,1)} %get-tuple-element.40.dylow_ref, bf16[1024,128]{1,0:T(8,128)(2,1)} %c_ref.5, f32[4,8,128,256]{3,2,1,0:T(8,128)} %get-tuple-element.41.into_ref, ...), custom_call_target="tpu_custom_call" | custom-call | flops 3000000000 | bytes 10000000 | tf_op jit(solution)/shard_map/forward/pallas_call | solution.py:482
  58.2 0.0 all-to-all-done.1
  58.2 3.8 %all-to-all-start.2 = ((f32[4,256,128]{2,1,0:T(8,128)}), f32[4,256,128]{2,1,0:T(8,128)S(1)}, u32[]{:S(2)}, u32[]{:S(2)}) async-start(f32[4,256,128]{2,1,0:T(8,128)} %bitcast.10), calls=%async_computation.2 | async-start | bytes 1048576 | tf_op jit(solution)/shard_map/all_to_all | solution.py:500
  62.1 6.4 %backward.1 = (f32[4,8,128]{2,1,0:T(8,128)}, f32[256,128]{1,0:T(8,128)}, f32[256,128]{1,0:T(8,128)}, f32[256,128]{1,0:T(8,128)}, f32[256,128]{1,0:T(8,128)}) custom-call(bf16[4,1024,256]{2,1,0:T(8,128)(2,1)} %get-tuple-element.54.xhigh_ref, bf16[4,1024,256]{2,1,0:T(8,128)(2,1)} %get-tuple-element.55.xlow_ref, f32[4,8,256]{2,1,0:T(8,128)} %get-tuple-element.42.decay_ref, ...), custom_call_target="tpu_custom_call" | custom-call | flops 3000000000 | bytes 10000000 | tf_op jit(solution)/shard_map/backward/pallas_call | solution.py:503
  68.4 2.1 %collective-permute-start.3 = (f32[256,128]{1,0:T(8,128)}, f32[256,128]{1,0:T(8,128)S(1)}, u32[]{:S(2)}, u32[]{:S(2)}) collective-permute-start(f32[256,128]{1,0:T(8,128)} %get-tuple-element.62), channel_id=1, source_target_pairs={{0,1},{1,2},{2,3},{3,0},{4,5},{5,6},{6,7},{7,4},{8,9},{9,10},{10,1... | collective-permute-start | bytes 393224 | tf_op jit(solution)/shard_map/ppermute | solution.py:398
  70.5 1.3 %collective-permute-start.4 = (f32[256,128]{1,0:T(8,128)}, f32[256,128]{1,0:T(8,128)S(1)}, u32[]{:S(2)}, u32[]{:S(2)}) collective-permute-start(f32[256,128]{1,0:T(8,128)} %get-tuple-element.63), channel_id=1, source_target_pairs={{0,3},{1,0},{2,1},{3,2},{4,7},{5,4},{6,5},{7,6},{8,11},{9,8},{10,9... | collective-permute-start | bytes 393224 | tf_op jit(solution)/shard_map/ppermute | solution.py:398
  71.8 2.2 %collective-permute-start.5 = (f32[256,128]{1,0:T(8,128)}, f32[256,128]{1,0:T(8,128)S(1)}, u32[]{:S(2)}, u32[]{:S(2)}) collective-permute-start(f32[256,128]{1,0:T(8,128)} %get-tuple-element.64), channel_id=1, source_target_pairs={{0,2},{1,3},{2,0},{3,1},{4,6},{5,7},{6,4},{7,5},{8,10},{9,11},{10,... | collective-permute-start | bytes 393224 | tf_op jit(solution)/shard_map/ppermute | solution.py:398
  74.0 7.7 %last.1 = (bf16[1024,1024]{1,0:T(8,128)(2,1)}, f32[16,1024]{1,0:T(8,128)}) custom-call(bf16[1024,1024]{1,0:T(8,128)(2,1)} %x_ref.3, bf16[1024,128]{1,0:T(8,128)(2,1)} %b_ref.3, bf16[1024,128]{1,0:T(8,128)(2,1)} %get-tuple-element.35.scales_ref, f32[4,24,1024]{2,1,0:T(8,128)} %get-tuple-element.36.info_ref, f32[4,1024,256]{2,1,0:T(8,128)} %get-tuple-element.37.adj_ref, ...), custom_call_target="tpu_custom_call" | custom-call | flops 3000000000 | bytes 10000000 | tf_op jit(solution)/shard_map/last/pallas_call | solution.py:520
  81.8 0.7 reduce_sum.9
  82.5 0.7 add_add_fusion
  (12 shorter events, 0.0 us)
Async XLA Ops:
  7.3 24.3 %all-to-all-start = ((f32[32,72,128]{2,1,0:T(8,128)}), f32[32,72,128]{2,1,0:T(8,128)S(1)}, u32[]{:S(2)}, u32[]{:S(2)}) async-start(f32[32,72,128]{2,1,0:T(8,128)} %get-tuple-element.43), calls=%async_computation | async-start | bytes 2359296 | tf_op jit(solution)/shard_map/all_to_all | solution.py:444
  32.7 25.5 %all-to-all-start.1 = ((f32[32,32,128]{2,1,0:T(8,128)}), f32[32,32,128]{2,1,0:T(8,128)S(1)}, u32[]{:S(2)}, u32[]{:S(2)}) async-start(f32[32,32,128]{2,1,0:T(8,128)} %get-tuple-element.53), calls=%async_computation.1 | async-start | bytes 1048576 | tf_op jit(solution)/shard_map/all_to_all | solution.py:481
  39.1 7.1 %collective-permute-start = (f32[8,32,128]{2,1,0:T(8,128)}, f32[8,32,128]{2,1,0:T(8,128)S(1)}, u32[]{:S(2)}, u32[]{:S(2)}) collective-permute-start(f32[8,32,128]{2,1,0:T(8,128)} %get-tuple-element.47), channel_id=1, source_target_pairs={{0,1},{1,2},{2,3},{3,0},{4,5},{5,6},{6,7},{7,4},{8,9},{9,10},{10,1... | collective-permute-start | bytes 393224 | tf_op jit(solution)/shard_map/ppermute | solution.py:398
  40.8 9.4 %collective-permute-start.1 = (f32[8,32,128]{2,1,0:T(8,128)}, f32[8,32,128]{2,1,0:T(8,128)S(1)}, u32[]{:S(2)}, u32[]{:S(2)}) collective-permute-start(f32[8,32,128]{2,1,0:T(8,128)} %get-tuple-element.48), channel_id=1, source_target_pairs={{0,2},{1,3},{2,0},{3,1},{4,6},{5,7},{6,4},{7,5},{8,10},{9,11},{10,... | collective-permute-start | bytes 393224 | tf_op jit(solution)/shard_map/ppermute | solution.py:398
  43.7 6.5 %collective-permute-start.2 = (f32[8,32,128]{2,1,0:T(8,128)}, f32[8,32,128]{2,1,0:T(8,128)S(1)}, u32[]{:S(2)}, u32[]{:S(2)}) collective-permute-start(f32[8,32,128]{2,1,0:T(8,128)} %get-tuple-element.49), channel_id=1, source_target_pairs={{0,3},{1,0},{2,1},{3,2},{4,7},{5,4},{6,5},{7,6},{8,11},{9,8},{10,9... | collective-permute-start | bytes 393224 | tf_op jit(solution)/shard_map/ppermute | solution.py:398
  46.2 4.0 %copy-start.2 = (f32[8,32,128]{2,1,0:T(8,128)}, f32[8,32,128]{2,1,0:T(8,128)S(1)}, u32[]{:S(2)}) copy-start(f32[8,32,128]{2,1,0:T(8,128)S(1)} %collective-permute-done.start1_ref) | copy-start | bytes 393220
  50.2 0.6 copy-start.3
  50.2 0.7 copy-start.4
  58.2 3.8 %copy-start = (f32[32,32,128]{2,1,0:T(8,128)}, f32[32,32,128]{2,1,0:T(8,128)S(1)}, u32[]{:S(2)}) copy-start(f32[32,32,128]{2,1,0:T(8,128)S(1)} %all-to-all-done.1) | copy-start | bytes 1572868
  58.2 23.5 %all-to-all-start.2 = ((f32[4,256,128]{2,1,0:T(8,128)}), f32[4,256,128]{2,1,0:T(8,128)S(1)}, u32[]{:S(2)}, u32[]{:S(2)}) async-start(f32[4,256,128]{2,1,0:T(8,128)} %bitcast.10), calls=%async_computation.2 | async-start | bytes 1048576 | tf_op jit(solution)/shard_map/all_to_all | solution.py:500
  68.4 14.0 %collective-permute-start.3 = (f32[256,128]{1,0:T(8,128)}, f32[256,128]{1,0:T(8,128)S(1)}, u32[]{:S(2)}, u32[]{:S(2)}) collective-permute-start(f32[256,128]{1,0:T(8,128)} %get-tuple-element.62), channel_id=1, source_target_pairs={{0,1},{1,2},{2,3},{3,0},{4,5},{5,6},{6,7},{7,4},{8,9},{9,10},{10,1... | collective-permute-start | bytes 393224 | tf_op jit(solution)/shard_map/ppermute | solution.py:398
  70.5 12.0 %collective-permute-start.4 = (f32[256,128]{1,0:T(8,128)}, f32[256,128]{1,0:T(8,128)S(1)}, u32[]{:S(2)}, u32[]{:S(2)}) collective-permute-start(f32[256,128]{1,0:T(8,128)} %get-tuple-element.63), channel_id=1, source_target_pairs={{0,3},{1,0},{2,1},{3,2},{4,7},{5,4},{6,5},{7,6},{8,11},{9,8},{10,9... | collective-permute-start | bytes 393224 | tf_op jit(solution)/shard_map/ppermute | solution.py:398
  71.8 10.7 %collective-permute-start.5 = (f32[256,128]{1,0:T(8,128)}, f32[256,128]{1,0:T(8,128)S(1)}, u32[]{:S(2)}, u32[]{:S(2)}) collective-permute-start(f32[256,128]{1,0:T(8,128)} %get-tuple-element.64), channel_id=1, source_target_pairs={{0,2},{1,3},{2,0},{3,1},{4,6},{5,7},{6,4},{7,5},{8,10},{9,11},{10,... | collective-permute-start | bytes 393224 | tf_op jit(solution)/shard_map/ppermute | solution.py:398
  74.0 8.4 %copy-start.1 = (f32[256,128]{1,0:T(8,128)S(1)}, f32[256,128]{1,0:T(8,128)}, u32[]{:S(2)}) copy-start(f32[256,128]{1,0:T(8,128)} %get-tuple-element.61) | copy-start | bytes 393220
